TPU v7x, 32 devices: a whole 2x2x4 slice. The times are simulated.
32 devices in a mesh: lam: 16 (over z, x, core), atom: 2 (over y).
Axes of the slice: x: 2, y: 2, z: 4, core: 2. Of those that a mesh axis runs over, the one named last changes fastest.
Arguments:
- coords: float32 [16, 3, 16384], P('lam', None, 'atom'), may hold values from 0 to 1
- velocities: float32 [16, 3, 16384], P('lam', None, 'atom'), may hold values from -6 to 6
- coupling: float32 [16, 2, 16384], P('lam', None, 'atom'), may hold values from 0.2 to 1
- charges: float32 [16384], replicated, may hold values from -1.5 to 1.5
- types: int32 [16384], replicated, may hold values from 0 to 15
- type_sigma: float32 [16], replicated, may hold values from 0.25 to 0.4
- type_eps: float32 [16], replicated, may hold values from 0.1 to 1
- near_tiles: int32 [128, 5], P('atom'), may hold values from 0 to 127
- accept: int32 [16], replicated, may hold values from 0 to 1, as said below
Outputs:
- energies: float32 [16, 3], P('lam')
- forces: float32 [16, 3, 16384], P('lam', None, 'atom')
- new_coords: float32 [16, 3, 16384], P('lam', None, 'atom')
- new_velocities: float32 [16, 3, 16384], P('lam', None, 'atom')
Inputs may be any that keep to these rules, and one draw needn't show every extreme that they name: accept[r] = 1 exchanges replicas r and r + 1 (modulo 16); no two consecutive entries around the cycle are both 1.
All inputs are finite; a program needn't handle non-finite values.
Results may differ from a plain program's by a relative error of at most 0.0003.
Values sent between devices are 32-bit elements; how exact they have to be, the bound alone decides.
A program may use at most 64 MiB of HBM per device.

v0:
```python
from functools import partial

import jax
import jax.numpy as jnp
from jax import lax
from jax.experimental import pallas as pl
from jax.experimental.pallas import tpu as pltpu
from jax.sharding import PartitionSpec as P

TILE = 128
DELTA_SOFT = 0.05
SUB = 8
DEPTH = 48


def moved(x, lam_by, atom_by):
    cycle, parts = lax.axis_size("lam"), lax.axis_size("atom")
    pairs = []
    for r in range(cycle):
        for a in range(parts):
            source = ((r - lam_by) % cycle) * parts + (a + atom_by) % parts
            pairs.append((source, r * parts + a))
    return lax.ppermute(x, ("lam", "atom"), pairs)


def split3(x):
    high = x.astype(jnp.bfloat16).astype(jnp.float32)
    rest = x - high
    mid = rest.astype(jnp.bfloat16).astype(jnp.float32)
    return high, mid, rest - mid


def lane_sums(ones, x):
    return lax.dot_general(
        ones, x, (((1,), (1,)), ((), ())), preferred_element_type=jnp.float32
    )


def tiles_kernel(parts, listed, *refs):
    where_ref, near_ref, sigma_ref, eps_ref, charges_ref, types_ref = refs[:6]
    halves = refs[6 : 6 + 3 * parts]
    force_ref, energy_ref, cols, left, right, lbuf, rbuf = refs[6 + 3 * parts : 13 + 3 * parts]
    geos, owns, accs = [refs[13 + 3 * parts + 2 * i :][:2] for i in range(3)]
    width = halves[0].shape[2]
    atoms = cols.shape[1]
    row_tiles = width // TILE
    part = where_ref[0]
    first_tile = part * row_tiles

    kinds = types_ref[...]
    radius = jnp.zeros(kinds.shape, jnp.float32)
    depth = jnp.zeros(kinds.shape, jnp.float32)
    for level in range(sigma_ref.shape[0]):
        here = kinds == level
        radius = jnp.where(here, sigma_ref[level], radius)
        depth = jnp.where(here, eps_ref[level], depth)
    cols[3:4, :] = 0.5 * radius
    cols[10:16, :] = jnp.zeros((6, atoms), jnp.float32)
    base = 2.0 * jnp.sqrt(depth)
    spans = []
    for step in range(parts):
        start = pl.multiple_of(lax.rem(part + step, parts) * width, TILE)
        spans.append(pl.ds(start, width))
        cols[0:3, spans[step]] = halves[step][0, 0:3] - 0.5
    for h in range(3):
        for step in range(parts):
            block = halves[parts * h + step]
            last = block.shape[1]
            cols[4 + 2 * h : 6 + 2 * h, spans[step]] = block[0, last - 2 : last]
        cols[4 + 2 * h : 5 + 2 * h, :] = cols[4 + 2 * h : 5 + 2 * h, :] * charges_ref[...]
        cols[5 + 2 * h : 6 + 2 * h, :] = cols[5 + 2 * h : 6 + 2 * h, :] * base

    chunk = lbuf.shape[1]
    lbuf[...] = jnp.zeros(lbuf.shape, jnp.float32)
    rbuf[...] = jnp.zeros(rbuf.shape, jnp.float32)
    lbuf[30:39, :] = jnp.ones((9, chunk), jnp.float32)
    rbuf[24:30, :] = jnp.ones((6, chunk), jnp.float32)
    soft_parts = split3(jnp.full((1, chunk), DELTA_SOFT, jnp.float32))
    for i in range(3):
        rbuf[36 + i : 37 + i, :] = soft_parts[i]
    row = lax.broadcasted_iota(jnp.int32, (DEPTH, TILE), 0)
    cross = row < 24
    radial = cross & (lax.rem(row, 4) == 3) | ((row >= 27) & (row < 30)) | ((row >= 33) & (row < 36))
    keep_u = (~radial) & (row < 39)
    keep_v = row < 36
    keeps = (keep_u, keep_v, radial)
    quad = lax.broadcasted_iota(jnp.int32, (4, chunk), 0)
    sign = jnp.where(quad == 3, 2.0, -2.0).astype(jnp.float32)

    def prepare(c, carry):
        span = pl.ds(pl.multiple_of(c * chunk, TILE), chunk)
        four = cols[0:4, span]
        square = four * four
        norm = split3(square[0:1] + square[1:2] + square[2:3])
        area = split3(square[3:4])
        high, mid, low = split3(four)
        shigh, smid, slow = high * sign, mid * sign, low * sign
        for i, v in enumerate((high, high, mid, mid, high, low)):
            lbuf[4 * i : 4 * i + 4, :] = v
        for i, v in enumerate((shigh, smid, shigh, smid, slow, shigh)):
            rbuf[4 * i : 4 * i + 4, :] = v
        for i in range(3):
            lbuf[24 + i : 25 + i, :] = norm[i]
            lbuf[27 + i : 28 + i, :] = area[i]
            rbuf[30 + i : 31 + i, :] = norm[i]
            rbuf[33 + i : 34 + i, :] = area[i]
        charge = split3(cols[4:5, span])
        well = split3(6.0 * cols[5:6, span])
        for i in range(3):
            lbuf[40 + i : 41 + i, :] = charge[i]
            lbuf[43 + i : 44 + i, :] = well[i]
        left[:, span] = lbuf[...]
        for i in range(chunk // TILE):
            block = rbuf[:, i * TILE : (i + 1) * TILE]
            for j in range(3):
                place = pl.multiple_of((c * (chunk // TILE) + i) * (3 * TILE) + j * TILE, TILE)
                right[:, pl.ds(place, TILE)] = jnp.where(keeps[j], block, 0.0).astype(jnp.bfloat16)
        return carry

    lax.fori_loop(0, atoms // chunk, prepare, 0)

    side = lax.broadcasted_iota(jnp.int32, (DEPTH, 2 * TILE), 1) < TILE
    deep = lax.broadcasted_iota(jnp.int32, (DEPTH, 2 * TILE), 0)
    spread = jnp.where(
        side & (deep >= 40) & (deep < 43) | (~side) & (deep >= 43) & (deep < 46), 1.0, 0.0
    ).astype(jnp.bfloat16)
    ones = jnp.ones((SUB, 2 * TILE), jnp.bfloat16)

    def geometry(t, s):
        own_span = pl.ds(pl.multiple_of((first_tile + t) * TILE, TILE), TILE)
        lhs = left[:, own_span].T.astype(jnp.bfloat16)
        owns[s][...] = jnp.dot(lhs, spread, preferred_element_type=jnp.float32)
        for k in range(listed):
            span = pl.ds(pl.multiple_of(near_ref[t, k] * (3 * TILE), TILE), 3 * TILE)
            geos[s][k] = jnp.dot(lhs, right[:, span], preferred_element_type=jnp.float32)

    def blocks(t, s, selfs):
        own = first_tile + t
        own_span = pl.ds(pl.multiple_of(own * TILE, TILE), TILE)
        near = [near_ref[t, k] for k in range(listed)]
        near_spans = [pl.ds(pl.multiple_of(n * TILE, TILE), TILE) for n in near]
        twice = jnp.float32(0.0)
        for n in near:
            twice = twice + (n == own).astype(jnp.float32)
        mine = cols[:, own_span]
        selfs = selfs + twice * (mine * mine)
        for b in range(TILE // SUB):
            rows = pl.ds(b * SUB, SUB)
            qi = owns[s][rows, 0:TILE]
            e6 = owns[s][rows, TILE : 2 * TILE]
            sums = [None] * 10

            def put(slot, value):
                sums[slot] = value if sums[slot] is None else sums[slot] + value

            for k, span in enumerate(near_spans):
                def col(c):
                    return jnp.broadcast_to(cols[c : c + 1, span], (SUB, TILE))

                inv = lax.rsqrt(geos[s][k, rows, 0:TILE])
                root = lax.rsqrt(geos[s][k, rows, TILE : 2 * TILE])
                p = root * root
                x = geos[s][k, rows, 2 * TILE : 3 * TILE] * p
                x3 = x * x * x
                low = x3 - 1.0
                lj = x3 * low
                charge = col(4) * inv
                put(4, charge)
                put(5, col(5) * lj)
                put(6, col(6) * inv)
                put(7, col(7) * lj)
                put(8, col(8) * inv)
                put(9, col(9) * lj)
                w = qi * (charge * (inv * inv)) + (e6 * col(5)) * ((x3 * p) * (x3 + low))
                put(0, w * col(0))
                put(1, w * col(1))
                put(2, w * col(2))
                put(3, w)
            for c in range(10):
                accs[s][c, rows, :] = sums[c]
        return selfs

    def finish(t, s, totals):
        own_span = pl.ds(pl.multiple_of((first_tile + t) * TILE, TILE), TILE)
        flat = []
        for c in range(0, 10, 2):
            pair = []
            for whole in (accs[s][c], accs[s][c + 1]):
                high = whole.astype(jnp.bfloat16)
                rest = (whole - high.astype(jnp.float32)).astype(jnp.bfloat16)
                pair.append(jnp.concatenate([high, rest], axis=1))
            both = lane_sums(ones, jnp.concatenate(pair, axis=0))
            flat += [both[0:1, :TILE], both[0:1, TILE:]]
        mine = cols[:, own_span]
        out_span = pl.ds(pl.multiple_of(t * TILE, TILE), TILE)
        for c in range(3):
            force_ref[0, c : c + 1, out_span] = mine[c : c + 1] * flat[3] - flat[c]
        return tuple(
            totals[h]
            + (mine[4 + 2 * h : 5 + 2 * h] * flat[4 + 2 * h] + mine[5 + 2 * h : 6 + 2 * h] * flat[5 + 2 * h])
            for h in range(3)
        )

    def two_tiles(m, carry):
        totals, selfs = carry
        t = 2 * m
        totals = finish(jnp.maximum(t - 1, 0), 1, totals)
        geometry(t + 1, 1)
        selfs = blocks(t, 0, selfs)
        totals = finish(t, 0, totals)
        geometry(jnp.minimum(t + 2, row_tiles - 1), 0)
        selfs = blocks(t + 1, 1, selfs)
        return totals, selfs

    zero = jnp.zeros((16, TILE), jnp.float32)
    none = jnp.zeros((1, TILE), jnp.float32)
    accs[1][...] = jnp.zeros(accs[1].shape, jnp.float32)
    geometry(0, 0)
    totals, selfs = lax.fori_loop(0, row_tiles // 2, two_tiles, ((none,) * 3, zero))
    totals = finish(row_tiles - 1, 1, totals)
    soft = lax.rsqrt(jnp.full((1, TILE), DELTA_SOFT, jnp.float32))
    lane1 = lax.broadcasted_iota(jnp.int32, (1, TILE), 1)
    line = jnp.zeros((1, TILE), jnp.float32)
    for h in range(3):
        c = 4 + 2 * h
        value = jnp.sum(totals[h] - selfs[c : c + 1] * soft)
        line = jnp.where(lane1 == h, value, line)
    energy_ref[...] = line


def per_device(
    coords, velocities, coupling, charges, types, type_sigma, type_eps, near_tiles, accept
):
    parts, width = lax.axis_size("atom"), coords.shape[2]
    atoms = parts * width
    part = lax.axis_index("atom")
    packed = jnp.concatenate([coords, velocities, coupling], axis=1)
    rows = jnp.concatenate([coords, coupling], axis=1)
    lower, upper = moved(packed, 1, 0), moved(packed, -1, 0)
    halves = [rows] + [moved(rows, 0, step) for step in range(1, parts)]
    for by, block in ((1, lower), (-1, upper)):
        halves.append(block)
        for step in range(1, parts):
            halves.append(moved(coupling, by, step))

    smem = pl.BlockSpec(memory_space=pltpu.SMEM)
    vmem = pl.BlockSpec(memory_space=pltpu.VMEM)
    pairs = width * near_tiles.shape[1] * TILE
    force, line = pl.pallas_call(
        partial(tiles_kernel, parts, near_tiles.shape[1]),
        out_shape=(
            jax.ShapeDtypeStruct(coords.shape, jnp.float32),
            jax.ShapeDtypeStruct((1, TILE), jnp.float32),
        ),
        in_specs=[smem] * 4 + [vmem] * (2 + len(halves)),
        out_specs=(vmem, vmem),
        scratch_shapes=[
            pltpu.VMEM((16, atoms), jnp.float32),
            pltpu.VMEM((DEPTH, atoms), jnp.float32),
            pltpu.VMEM((DEPTH, 3 * atoms), jnp.bfloat16),
            pltpu.VMEM((DEPTH, 4 * TILE), jnp.float32),
            pltpu.VMEM((DEPTH, 4 * TILE), jnp.float32),
        ]
        + [pltpu.VMEM((near_tiles.shape[1], TILE, 3 * TILE), jnp.float32)] * 2
        + [pltpu.VMEM((TILE, 2 * TILE), jnp.float32)] * 2
        + [pltpu.VMEM((10, TILE, TILE), jnp.float32)] * 2,
        cost_estimate=pl.CostEstimate(
            flops=50 * pairs, bytes_accessed=4 * 20 * atoms, transcendentals=2 * pairs
        ),
        name="tiles",
    )(
        part.reshape(1).astype(jnp.int32),
        near_tiles,
        type_sigma,
        type_eps,
        charges.reshape(1, atoms),
        types.reshape(1, atoms),
        *halves,
    )
    shares = jnp.stack([line[0, :3]] + [moved(line, 0, step)[0, :3] for step in range(1, parts)])
    total = shares[0]
    for step in range(1, parts):
        total = total + shares[step]
    if parts > 2:
        order = (jnp.arange(parts) - part) % parts
        total = jnp.sum(shares[order], axis=0)
    energies = (total * (0.5 / atoms))[None]

    replica, cycle = lax.axis_index("lam"), lax.axis_size("lam")
    up = accept[replica] == 1
    low = accept[(replica + cycle - 1) % cycle] == 1
    new_coords = jnp.where(up, upper[:, 0:3], jnp.where(low, lower[:, 0:3], coords))
    new_velocities = jnp.where(up, upper[:, 3:6], jnp.where(low, lower[:, 3:6], velocities))
    return (energies, force, new_coords, new_velocities)


def solution(mesh):
    split = P("lam", None, "atom")
    return jax.shard_map(
        per_device,
        mesh=mesh,
        in_specs=(split, split, split, P(), P(), P(), P(), P("atom", None), P()),
        out_specs=(P("lam", None), split, split, split),
        check_vma=False,
    )
```

profile of v0, /device:TPU:0, one launch (start us, length us, event | category | flops | bytes accessed | tf_op | source)
XLA Modules:
  0.0 73.1 jit_solution(3106498065340281436)
XLA Ops:
  0.6 1.0 %copy.13 = f32[1,3,8192]{2,1,0:T(4,128)S(1)} copy(f32[1,3,8192]{2,0,1:T(1,128)} %param.9) | data formatting | bytes 196608 | tf_op args[0]
  1.7 0.1 copy.15
  1.7 0.8 %copy-done.4 = f32[1,2,8192]{2,1,0:T(2,128)S(1)} copy-done((f32[1,2,8192]{2,1,0:T(2,128)S(1)}, f32[1,2,8192]{2,1,0:T(2,128)}, u32[]{:S(2)}) %copy-start.4) | copy-done | bytes 65560
  2.5 0.1 pad_maximum_fusion.1
  2.6 0.5 collective-permute-start.1
  3.1 5.0 %collective-permute-start.3 = (f32[1,8,8192]{2,1,0:T(8,128)S(1)}, f32[1,8,8192]{2,1,0:T(8,128)S(1)}, u32[]{:S(2)}, u32[]{:S(2)}) collective-permute-start(f32[1,8,8192]{2,1,0:T(8,128)S(1)} %pad_maximum_fusion.1), channel_id=1, source_target_pairs={{2,0},{3,1},{4,2},{5,3},{6,4},{7,5},{8,6},{9,7},{10,8},{11,9},{12,... | collective-permute-start | bytes 786440 | tf_op jit(solution)/shard_map/ppermute | solution.py:23
  8.2 0.1 pad_maximum_fusion.refs_6_
  8.2 2.0 %collective-permute-start = (f32[1,5,8192]{2,1,0:T(8,128)S(1)}, f32[1,5,8192]{2,1,0:T(8,128)S(1)}, u32[]{:S(2)}, u32[]{:S(2)}) collective-permute-start(f32[1,5,8192]{2,1,0:T(8,128)S(1)} %pad_maximum_fusion.refs_6_), channel_id=1, source_target_pairs={{1,0},{0,1},{3,2},{2,3},{5,4},{4,5},{7,6},{6,7},{9,8},{8,9},{11,10... | collective-permute-start | bytes 491528 | tf_op jit(solution)/shard_map/ppermute | solution.py:23
  10.2 5.3 %collective-permute-start.4 = (f32[1,2,8192]{2,1,0:T(2,128)S(1)}, f32[1,2,8192]{2,1,0:T(2,128)S(1)}, u32[]{:S(2)}, u32[]{:S(2)}) collective-permute-start(f32[1,2,8192]{2,1,0:T(2,128)S(1)} %copy-done.4), channel_id=1, source_target_pairs={{3,0},{2,1},{5,2},{4,3},{7,4},{6,5},{9,6},{8,7},{11,8},{10,9},{13,... | collective-permute-start | bytes 196616 | tf_op jit(solution)/shard_map/ppermute | solution.py:23
  15.6 0.7 copy-done.7
  16.2 0.7 copy.16.refs_1_
  17.0 0.6 fusion.2
  19.0 0.5 copy-done.10
  19.5 0.1 copy-done.9
  19.6 0.1 copy-done.2
  19.7 0.1 copy-done.3
  19.8 48.3 %tiles.1 = (f32[1,3,8192]{2,1,0:T(4,128)}, f32[1,128]{1,0:T(1,128)}) custom-call(s32[1]{0:T(128)} %bitcast.refs_0_, s32[64,5]{1,0:T(8,128)} %copy.16.refs_1_, f32[16]{0:T(128)} %refs_2_.1, f32[16]{0:T(128)} %refs_3_.1, f32[1,16384]{1,0:T(1,128)} %bitcast.5, s32[1,16384]{1,0:T(1,128)} %bitcast.6, f32[1,5,8192]{2,1,0:T(8,128)} %copy-done.5, ...), custom_call_target="tpu_custom_call" | custom-call | flops 262144000 | bytes 1310720 | tf_op jit(solution)/shard_map/tiles/pallas_call | solution.py:249
  68.1 0.6 copy-done.12
  68.7 0.2 collective-permute-start.5
  68.9 1.5 %fusion = (f32[1,3,8192]{2,1,0:T(4,128)S(1)}, f32[1,3,8192]{2,1,0:T(4,128)S(1)}) fusion(f32[1,8,8192]{2,1,0:T(8,128)} %copy-done.2, f32[1,8,8192]{2,1,0:T(8,128)} %copy-done.3, pred[]{:T(512)} %bitcast.4, pred[]{:T(512)} %bitcast.3, f32[1,3,8192]{2,0,1:T(1,128)S(1)} %copy-done.1, f32[1,3,8192]{2,0,1:T(1,128)S(1)} %copy-done), kind=kLoop, calls=%fused_computation.3 | loop fusion | flops 98304 | bytes 786434 | tf_op jit(solution)/shard_map/jit(_where)/select_n | solution.py:293
  70.3 0.7 %copy.19 = f32[1,3,8192]{2,0,1:T(1,128)} copy(f32[1,3,8192]{2,1,0:T(4,128)S(1)} %copy-done.6) | data formatting | bytes 196608
  71.1 0.7 %copy.20 = f32[1,3,8192]{2,0,1:T(1,128)} copy(f32[1,3,8192]{2,1,0:T(4,128)S(1)} %get-tuple-element.13) | data formatting | bytes 196608
  71.8 0.7 %copy.21 = f32[1,3,8192]{2,0,1:T(1,128)} copy(f32[1,3,8192]{2,1,0:T(4,128)S(1)} %get-tuple-element.12) | data formatting | bytes 196608
  72.6 0.5 add_multiply_fusion
  (26 shorter events, 0.1 us)
Async XLA Ops:
  0.6 1.0 %copy-start.1 = (f32[1,3,8192]{2,0,1:T(1,128)S(1)}, f32[1,3,8192]{2,0,1:T(1,128)}, u32[]{:S(2)}) copy-start(f32[1,3,8192]{2,0,1:T(1,128)} %param.10) | copy-start | bytes 294916
  1.7 0.8 %copy-start.4 = (f32[1,2,8192]{2,1,0:T(2,128)S(1)}, f32[1,2,8192]{2,1,0:T(2,128)}, u32[]{:S(2)}) copy-start(f32[1,2,8192]{2,1,0:T(2,128)} %param.11) | copy-start | bytes 196612
  2.6 16.3 %collective-permute-start.1 = (f32[1,8,8192]{2,1,0:T(8,128)S(1)}, f32[1,8,8192]{2,1,0:T(8,128)S(1)}, u32[]{:S(2)}, u32[]{:S(2)}) collective-permute-start(f32[1,8,8192]{2,1,0:T(8,128)S(1)} %pad_maximum_fusion.1), channel_id=1, source_target_pairs={{30,0},{31,1},{0,2},{1,3},{2,4},{3,5},{4,6},{5,7},{6,8},{7,9},{8,1... | collective-permute-start | bytes 786440 | tf_op jit(solution)/shard_map/ppermute | solution.py:23
  3.1 15.8 %collective-permute-start.3 = (f32[1,8,8192]{2,1,0:T(8,128)S(1)}, f32[1,8,8192]{2,1,0:T(8,128)S(1)}, u32[]{:S(2)}, u32[]{:S(2)}) collective-permute-start(f32[1,8,8192]{2,1,0:T(8,128)S(1)} %pad_maximum_fusion.1), channel_id=1, source_target_pairs={{2,0},{3,1},{4,2},{5,3},{6,4},{7,5},{8,6},{9,7},{10,8},{11,9},{12,... | collective-permute-start | bytes 786440 | tf_op jit(solution)/shard_map/ppermute | solution.py:23
  8.2 10.7 %copy-start.5 = (f32[1,5,8192]{2,1,0:T(8,128)}, f32[1,5,8192]{2,1,0:T(8,128)S(1)}, u32[]{:S(2)}) copy-start(f32[1,5,8192]{2,1,0:T(8,128)S(1)} %pad_maximum_fusion.refs_6_) | copy-start | bytes 491524
  8.2 10.7 %collective-permute-start = (f32[1,5,8192]{2,1,0:T(8,128)S(1)}, f32[1,5,8192]{2,1,0:T(8,128)S(1)}, u32[]{:S(2)}, u32[]{:S(2)}) collective-permute-start(f32[1,5,8192]{2,1,0:T(8,128)S(1)} %pad_maximum_fusion.refs_6_), channel_id=1, source_target_pairs={{1,0},{0,1},{3,2},{2,3},{5,4},{4,5},{7,6},{6,7},{9,8},{8,9},{11,10... | collective-permute-start | bytes 491528 | tf_op jit(solution)/shard_map/ppermute | solution.py:23
  10.2 8.6 %collective-permute-start.2 = (f32[1,2,8192]{2,1,0:T(2,128)S(1)}, f32[1,2,8192]{2,1,0:T(2,128)S(1)}, u32[]{:S(2)}, u32[]{:S(2)}) collective-permute-start(f32[1,2,8192]{2,1,0:T(2,128)S(1)} %copy-done.4), channel_id=1, source_target_pairs={{31,0},{30,1},{1,2},{0,3},{3,4},{2,5},{5,6},{4,7},{7,8},{6,9},{9,1... | collective-permute-start | bytes 196616 | tf_op jit(solution)/shard_map/ppermute | solution.py:23
  10.2 8.7 %collective-permute-start.4 = (f32[1,2,8192]{2,1,0:T(2,128)S(1)}, f32[1,2,8192]{2,1,0:T(2,128)S(1)}, u32[]{:S(2)}, u32[]{:S(2)}) collective-permute-start(f32[1,2,8192]{2,1,0:T(2,128)S(1)} %copy-done.4), channel_id=1, source_target_pairs={{3,0},{2,1},{5,2},{4,3},{7,4},{6,5},{9,6},{8,7},{11,8},{10,9},{13,... | collective-permute-start | bytes 196616 | tf_op jit(solution)/shard_map/ppermute | solution.py:23
  15.6 0.7 copy-start.7
  16.2 0.7 copy-start.8
  18.9 0.6 copy-start.10
  18.9 0.6 copy-start.11
  18.9 0.7 copy-start.9
  18.9 0.8 %copy-start.2 = (f32[1,8,8192]{2,1,0:T(8,128)}, f32[1,8,8192]{2,1,0:T(8,128)S(1)}, u32[]{:S(2)}) copy-start(f32[1,8,8192]{2,1,0:T(8,128)S(1)} %collective-permute-done.1.refs_8_) | copy-start | bytes 786436
  18.9 0.8 %copy-start.3 = (f32[1,8,8192]{2,1,0:T(8,128)}, f32[1,8,8192]{2,1,0:T(8,128)S(1)}, u32[]{:S(2)}) copy-start(f32[1,8,8192]{2,1,0:T(8,128)S(1)} %collective-permute-done.3.refs_10_) | copy-start | bytes 786436
  19.8 49.1 %copy-start = (f32[1,3,8192]{2,0,1:T(1,128)S(1)}, f32[1,3,8192]{2,0,1:T(1,128)}, u32[]{:S(2)}) copy-start(f32[1,3,8192]{2,0,1:T(1,128)} %param.9) | copy-start | bytes 294916
  68.1 0.6 copy-start.12
  68.7 3.9 %collective-permute-start.5 = (f32[1,128]{1,0:T(1,128)S(1)}, f32[1,128]{1,0:T(1,128)S(1)}, u32[]{:S(2)}, u32[]{:S(2)}) collective-permute-start(f32[1,128]{1,0:T(1,128)S(1)} %copy-done.12), channel_id=1, source_target_pairs={{1,0},{0,1},{3,2},{2,3},{5,4},{4,5},{7,6},{6,7},{9,8},{8,9},{11,10... | collective-permute-start | bytes 1544 | tf_op jit(solution)/shard_map/ppermute | solution.py:23
  68.9 1.5 %copy-start.6 = (f32[1,3,8192]{2,1,0:T(4,128)S(1)}, f32[1,3,8192]{2,1,0:T(4,128)}, u32[]{:S(2)}) copy-start(f32[1,3,8192]{2,1,0:T(4,128)} %get-tuple-element.9) | copy-start | bytes 294916
where the time goes:
time: 73.4 us; the launch traced here: 73.1 us
  Pallas kernels  48.3 us (66%)
  starting transfers between devices  13.1 us (18%)
  local copies, waits for them, and re-layouts  7.5 us (10%)
  other arithmetic  2.12 us (3%)
  between operations  2.09 us (3%)
    pallas_call x1, Pallas kernels, per_device(): pl.pallas_call(partial(tiles_kernel, parts, near_tiles.shape[1]), out_sha...  48.3 us
    ppermute x6, starting transfers between devices, moved(): return lax.ppermute(x, ('lam', 'atom'), pairs)  13.1 us
    unnamed x32, local copies, waits for them, and re-layouts  6.91 us
  transfers between devices with their start and end apart: 6, of which 0 were waited for; matrix products, arithmetic and copies ran while one was open for 7% of the time, Pallas kernels for 0%

commit v1 on v0

v1 whole, which is shorter than its diff:
```python
from functools import partial

import jax
import jax.numpy as jnp
from jax import lax
from jax.experimental import pallas as pl
from jax.experimental.pallas import tpu as pltpu
from jax.sharding import PartitionSpec as P

TILE = 128
DELTA_SOFT = 0.05
SUB = 16
DEPTH = 32
COLS = 2
UNROLL = 2
GROUP = 8


def moved(x, lam_by, atom_by):
    cycle, parts = lax.axis_size("lam"), lax.axis_size("atom")
    pairs = []
    for r in range(cycle):
        for a in range(parts):
            source = ((r - lam_by) % cycle) * parts + (a + atom_by) % parts
            pairs.append((source, r * parts + a))
    return lax.ppermute(x, ("lam", "atom"), pairs)


def halved(x):
    high = x.astype(jnp.bfloat16)
    low = x - high.astype(jnp.float32)
    return jnp.concatenate([high, low.astype(jnp.bfloat16)], axis=1)


def rounded(x):
    return x.astype(jnp.bfloat16).astype(jnp.float32)


def tiles_kernel(parts, listed, *refs):
    where_ref, near_ref, sigma_ref, eps_ref, charges_ref, types_ref = refs[:6]
    halves = refs[6 : 6 + 3 * parts]
    rest = refs[6 + 3 * parts :]
    force_ref, energy_ref, cols, near_feat, own_feat, lhs_e, lhs_f = rest[:7]
    geos = rest[7 : 7 + UNROLL]
    sums = rest[7 + UNROLL : 7 + 2 * UNROLL]
    width = halves[0].shape[2]
    atoms = cols.shape[1]
    row_tiles = width // TILE
    part = where_ref[0]
    first_tile = part * row_tiles

    kinds = types_ref[...]
    radius = jnp.zeros(kinds.shape, jnp.float32)
    depth = jnp.zeros(kinds.shape, jnp.float32)
    for level in range(sigma_ref.shape[0]):
        here = kinds == level
        radius = jnp.where(here, sigma_ref[level], radius)
        depth = jnp.where(here, eps_ref[level], depth)
    cols[3:4, :] = 0.5 * radius
    cols[4:8, :] = jnp.zeros((4, atoms), jnp.float32)
    cols[11:12, :] = jnp.zeros((1, atoms), jnp.float32)
    cols[15:16, :] = jnp.zeros((1, atoms), jnp.float32)
    base = 2.0 * jnp.sqrt(depth)
    spans = []
    for step in range(parts):
        start = pl.multiple_of(lax.rem(part + step, parts) * width, TILE)
        spans.append(pl.ds(start, width))
        cols[0:3, spans[step]] = halves[step][0, 0:3] - 0.5
    for h in range(3):
        for step in range(parts):
            block = halves[parts * h + step]
            last = block.shape[1]
            cols[8 + h : 9 + h, spans[step]] = block[0, last - 2 : last - 1]
            cols[12 + h : 13 + h, spans[step]] = block[0, last - 1 : last]
        cols[8 + h : 9 + h, :] = cols[8 + h : 9 + h, :] * charges_ref[...]
        cols[12 + h : 13 + h, :] = cols[12 + h : 13 + h, :] * base

    def rows_of(n):
        return lax.broadcasted_iota(jnp.int32, (8, n), 0)

    def base_rows(span):
        four = cols[0:4, span]
        return jnp.concatenate([four, four], axis=0)

    def thirds(x):
        high = rounded(x)
        low = x - high
        mid = rounded(low)
        return high, mid, low - mid

    def near_part(c):
        span = pl.ds(pl.multiple_of(c * TILE, TILE), TILE)
        sub = rows_of(TILE)
        quad = sub % 4
        f8 = base_rows(span)
        high, mid, low = thirds(f8)
        sign = jnp.where(quad == 3, 2.0, -2.0).astype(jnp.float32)
        square = f8 * f8
        norm = square[0:1] + square[1:2] + square[2:3]
        mixed = jnp.where(sub < 3, norm, square[3:4])
        nh, nm, nl = thirds(mixed)
        last = jnp.where(quad == 0, nh, jnp.where(quad == 1, nm, nl))
        last = jnp.where(sub == 3, nh, jnp.where(sub == 4, nm, last))
        last = jnp.where(sub >= 5, 1.0, last)
        feats = jnp.concatenate([high * sign, mid * sign, jnp.where(sub < 4, high, low) * sign, last], axis=0)
        near_feat[span, :] = feats.T.astype(jnp.bfloat16)
        own8 = cols[8:16, span]
        oh = rounded(own8)
        lhs_e[:, span] = jnp.concatenate([oh, own8 - oh], axis=0).astype(jnp.bfloat16)
        pos = jnp.where(quad == 3, 1.0, f8)
        scale = jnp.where(sub < 4, own8[0:1], 6.0 * own8[4:5])
        wide = pos * scale
        wh = rounded(wide)
        lhs_f[:, span] = jnp.concatenate([wh, wide - wh], axis=0).astype(jnp.bfloat16)

    def near_parts(c, carry):
        for i in range(GROUP):
            near_part(GROUP * c + i)
        return carry

    lax.fori_loop(0, atoms // (GROUP * TILE), near_parts, 0)

    def own_part(c, carry):
        span = pl.ds(pl.multiple_of((first_tile + c) * TILE, TILE), TILE)
        sub = rows_of(TILE)
        quad = sub % 4
        f8 = base_rows(span)
        high, mid, low = thirds(f8)
        square = f8 * f8
        norm = square[0:1] + square[1:2] + square[2:3]
        first = jnp.where(sub < 4, high, mid)
        third = jnp.where(sub < 4, low, high)
        outs = []
        for which in range(COLS):
            const = (norm + DELTA_SOFT, norm + square[3:4], square[3:4])[which]
            ch, cm, cl = thirds(const)
            ones = sub < (3, 5, 5)[which]
            if which == 2:
                ones = (sub == 3) | (sub == 4)
            last = jnp.where(ones, 1.0, 0.0)
            last = jnp.where(sub == 5, ch, jnp.where(sub == 6, cm, jnp.where(sub == 7, cl, last)))
            keep = (quad != 3, quad <= 3, quad == 3)[which]
            a = jnp.where(keep, first, 0.0)
            outs.append(jnp.concatenate([a, a, jnp.where(keep, third, 0.0), last], axis=0))
        place = pl.ds(pl.multiple_of(c * (COLS * TILE), TILE), COLS * TILE)
        own_feat[:, place] = jnp.concatenate(outs, axis=1).astype(jnp.bfloat16)
        return carry

    lax.fori_loop(0, row_tiles, own_part, 0)

    def geometry(t, s):
        place = pl.ds(pl.multiple_of(t * (COLS * TILE), TILE), COLS * TILE)
        rhs = own_feat[:, place]
        for k in range(listed):
            span = pl.ds(pl.multiple_of(near_ref[t, k] * TILE, TILE), TILE)
            geos[s][k] = jnp.dot(near_feat[span, :], rhs, preferred_element_type=jnp.float32)

    def blocks(t, s):
        total = None
        for k in range(listed):
            span = pl.ds(pl.multiple_of(near_ref[t, k] * TILE, TILE), TILE)
            invs, charge, ljs, well = [], [], [], []
            for b in range(TILE // SUB):
                rows = pl.ds(b * SUB, SUB)
                inv = lax.rsqrt(geos[s][k, rows, 0:TILE])
                charge.append(halved(inv * (inv * inv)))
                invs.append(inv.astype(jnp.bfloat16))
            for b in range(TILE // SUB):
                rows = pl.ds(b * SUB, SUB)
                both = geos[s][k, rows, TILE : 2 * TILE]
                root = lax.rsqrt(both)
                p = root * root
                if COLS == 3:
                    x = geos[s][k, rows, 2 * TILE : 3 * TILE] * p
                else:
                    x = ((both - geos[s][k, rows, 0:TILE]) + DELTA_SOFT) * p
                x3 = x * x * x
                low = x3 - 1.0
                ljs.append((x3 * low).astype(jnp.bfloat16))
                well.append(halved((x3 * p) * (x3 + low)))
            le = lhs_e[:, span]
            lf = lhs_f[:, span]
            fc = jnp.dot(lf, jnp.concatenate(charge, axis=0), preferred_element_type=jnp.float32)
            fw = jnp.dot(lf, jnp.concatenate(well, axis=0), preferred_element_type=jnp.float32)
            pairs = jnp.concatenate([jnp.concatenate(invs, axis=0), jnp.concatenate(ljs, axis=0)], axis=1)
            en = jnp.dot(le, pairs, preferred_element_type=jnp.float32)
            new = (fc, fw, en)
            total = new if total is None else tuple(x + y for x, y in zip(total, new))
        for i, x in enumerate(total):
            sums[s][i] = x

    def finish(t, s, carry):
        totals, selfs = carry
        own = first_tile + t
        own_span = pl.ds(pl.multiple_of(own * TILE, TILE), TILE)
        out_span = pl.ds(pl.multiple_of(t * TILE, TILE), TILE)
        sub = rows_of(TILE)
        quad = sub % 4
        mine = cols[8:16, own_span]
        fold = []
        for i in range(2):
            x = sums[s][i, 0:8] + sums[s][i, 8:16]
            fold.append(x[:, :TILE] + x[:, TILE:])
        en = sums[s][2, 0:8] + sums[s][2, 8:16]
        totals = totals + mine * jnp.where(sub < 4, en[:, :TILE], en[:, TILE:])
        twice = jnp.float32(0.0)
        for k in range(listed):
            twice = twice + (near_ref[t, k] == own).astype(jnp.float32)
        selfs = selfs + twice * (mine * mine)
        pull = jnp.where(sub < 4, fold[0] * mine[0:1], fold[1] * mine[4:5])
        pull = pull[0:4] + pull[4:8]
        force_ref[0, :, out_span] = cols[0:3, own_span] * pull[3:4] - pull[0:3]
        return totals, selfs

    def step(m, carry):
        for s in range(UNROLL):
            t = UNROLL * m + s
            before = (s - 1) % UNROLL
            carry = finish(jnp.maximum(t - 1, 0), before, carry)
            geometry(jnp.minimum(t + 1, row_tiles - 1), (s + 1) % UNROLL)
            blocks(t, s)
        return carry

    zero = jnp.zeros((8, TILE), jnp.float32)
    sums[UNROLL - 1][...] = jnp.zeros(sums[UNROLL - 1].shape, jnp.float32)
    geometry(0, 0)
    carry = lax.fori_loop(0, row_tiles // UNROLL, step, (zero, zero))
    twice = jnp.float32(0.0)
    for k in range(listed):
        twice = twice + (near_ref[0, k] == first_tile).astype(jnp.float32)
    first = cols[8:16, pl.ds(pl.multiple_of(first_tile * TILE, TILE), TILE)]
    totals, selfs = finish(row_tiles - 1, UNROLL - 1, carry)
    selfs = selfs - twice * (first * first)
    soft = rounded(lax.rsqrt(jnp.full((8, TILE), DELTA_SOFT, jnp.float32)))
    sub = rows_of(TILE)
    both = totals - jnp.where(sub < 4, selfs * soft, 0.0)
    lane1 = lax.broadcasted_iota(jnp.int32, (1, TILE), 1)
    line = jnp.zeros((1, TILE), jnp.float32)
    for h in range(3):
        value = jnp.sum(both[h : h + 1] + both[4 + h : 5 + h])
        line = jnp.where(lane1 == h, value, line)
    energy_ref[...] = line


def per_device(
    coords, velocities, coupling, charges, types, type_sigma, type_eps, near_tiles, accept
):
    parts, width = lax.axis_size("atom"), coords.shape[2]
    atoms = parts * width
    part = lax.axis_index("atom")
    packed = jnp.concatenate([coords, velocities, coupling], axis=1)
    rows = jnp.concatenate([coords, coupling], axis=1)
    lower, upper = moved(packed, 1, 0), moved(packed, -1, 0)
    halves = [rows] + [moved(rows, 0, step) for step in range(1, parts)]
    for by, block in ((1, lower), (-1, upper)):
        halves.append(block)
        for step in range(1, parts):
            halves.append(moved(coupling, by, step))

    smem = pl.BlockSpec(memory_space=pltpu.SMEM)
    vmem = pl.BlockSpec(memory_space=pltpu.VMEM)
    pairs = width * near_tiles.shape[1] * TILE
    force, line = pl.pallas_call(
        partial(tiles_kernel, parts, near_tiles.shape[1]),
        out_shape=(
            jax.ShapeDtypeStruct(coords.shape, jnp.float32),
            jax.ShapeDtypeStruct((1, TILE), jnp.float32),
        ),
        in_specs=[smem] * 4 + [vmem] * (2 + len(halves)),
        out_specs=(vmem, vmem),
        scratch_shapes=[
            pltpu.VMEM((16, atoms), jnp.float32),
            pltpu.VMEM((atoms, DEPTH), jnp.bfloat16),
            pltpu.VMEM((DEPTH, COLS * width), jnp.bfloat16),
            pltpu.VMEM((16, atoms), jnp.bfloat16),
            pltpu.VMEM((16, atoms), jnp.bfloat16),
        ]
        + [pltpu.VMEM((near_tiles.shape[1], TILE, COLS * TILE), jnp.float32)] * UNROLL
        + [pltpu.VMEM((3, 16, 2 * TILE), jnp.float32)] * UNROLL,
        cost_estimate=pl.CostEstimate(
            flops=50 * pairs, bytes_accessed=4 * 20 * atoms, transcendentals=2 * pairs
        ),
        name="tiles",
    )(
        part.reshape(1).astype(jnp.int32),
        near_tiles,
        type_sigma,
        type_eps,
        charges.reshape(1, atoms),
        types.reshape(1, atoms),
        *halves,
    )
    shares = jnp.stack([line[0, :3]] + [moved(line, 0, step)[0, :3] for step in range(1, parts)])
    total = shares[0]
    for step in range(1, parts):
        total = total + shares[step]
    if parts > 2:
        order = (jnp.arange(parts) - part) % parts
        total = jnp.sum(shares[order], axis=0)
    energies = (total * (0.5 / atoms))[None]

    replica, cycle = lax.axis_index("lam"), lax.axis_size("lam")
    up = accept[replica] == 1
    low = accept[(replica + cycle - 1) % cycle] == 1
    new_coords = jnp.where(up, upper[:, 0:3], jnp.where(low, lower[:, 0:3], coords))
    new_velocities = jnp.where(up, upper[:, 3:6], jnp.where(low, lower[:, 3:6], velocities))
    return (energies, force, new_coords, new_velocities)


def solution(mesh):
    split = P("lam", None, "atom")
    return jax.shard_map(
        per_device,
        mesh=mesh,
        in_specs=(split, split, split, P(), P(), P(), P(), P("atom", None), P()),
        out_specs=(P("lam", None), split, split, split),
        check_vma=False,
    )
```

time: 73.4 us -> 53.9 us (0.73)
  Pallas kernels: 48.3 us -> 28.8 us
    pallas_call x1, Pallas kernels: 48.3 us -> 28.8 us  [per_device(): pl.pallas_call(partial(tiles_kernel, parts, near_tiles.shape[1]), out_sha...]
  transfers between devices with their start and end apart: 6 -> 6, of which waited for: 0 -> 0; matrix products, arithmetic and copies ran while one was open for 7% -> 9% of each run, Pallas kernels for 0% -> 0%
where the time goes in v1:
time: 53.9 us; the launch traced here: 53.6 us
  Pallas kernels  28.8 us (53%)
  starting transfers between devices  13 us (24%)
  local copies, waits for them, and re-layouts  7.5 us (14%)
  other arithmetic  2.12 us (4%)
  between operations  2.09 us (4%)
    pallas_call x1, Pallas kernels, per_device(): pl.pallas_call(partial(tiles_kernel, parts, near_tiles.shape[1]), out_sha...  28.8 us
    ppermute x6, starting transfers between devices, moved(): return lax.ppermute(x, ('lam', 'atom'), pairs)  13 us
    unnamed x32, local copies, waits for them, and re-layouts  6.91 us
    select_n x1, other arithmetic, per_device(): jnp.where(up, upper[:, 3:6], jnp.where(low, lower[:, 3:6], velocities))  1.46 us
  transfers between devices with their start and end apart: 6, of which 0 were waited for; matrix products, arithmetic and copies ran while one was open for 9% of the time, Pallas kernels for 0%

profile of v1, /device:TPU:0, one launch (start us, length us, event | category | flops | bytes accessed | tf_op | source)
XLA Modules:
  0.0 53.6 jit_solution(7847744539366287886)
XLA Ops:
  0.6 1.0 %copy.13 = f32[1,3,8192]{2,1,0:T(4,128)S(1)} copy(f32[1,3,8192]{2,0,1:T(1,128)} %param.9) | data formatting | bytes 196608 | tf_op args[0]
  1.7 0.1 copy.15
  1.7 0.8 %copy-done.4 = f32[1,2,8192]{2,1,0:T(2,128)S(1)} copy-done((f32[1,2,8192]{2,1,0:T(2,128)S(1)}, f32[1,2,8192]{2,1,0:T(2,128)}, u32[]{:S(2)}) %copy-start.4) | copy-done | bytes 65560
  2.5 0.1 pad_maximum_fusion.1
  2.6 0.5 %collective-permute-start.1 = (f32[1,8,8192]{2,1,0:T(8,128)S(1)}, f32[1,8,8192]{2,1,0:T(8,128)S(1)}, u32[]{:S(2)}, u32[]{:S(2)}) collective-permute-start(f32[1,8,8192]{2,1,0:T(8,128)S(1)} %pad_maximum_fusion.1), channel_id=1, source_target_pairs={{30,0},{31,1},{0,2},{1,3},{2,4},{3,5},{4,6},{5,7},{6,8},{7,9},{8,1... | collective-permute-start | bytes 786440 | tf_op jit(solution)/shard_map/ppermute | solution.py:26
  3.1 5.0 %collective-permute-start.3 = (f32[1,8,8192]{2,1,0:T(8,128)S(1)}, f32[1,8,8192]{2,1,0:T(8,128)S(1)}, u32[]{:S(2)}, u32[]{:S(2)}) collective-permute-start(f32[1,8,8192]{2,1,0:T(8,128)S(1)} %pad_maximum_fusion.1), channel_id=1, source_target_pairs={{2,0},{3,1},{4,2},{5,3},{6,4},{7,5},{8,6},{9,7},{10,8},{11,9},{12,... | collective-permute-start | bytes 786440 | tf_op jit(solution)/shard_map/ppermute | solution.py:26
  8.2 0.1 pad_maximum_fusion.refs_6_
  8.2 2.0 %collective-permute-start = (f32[1,5,8192]{2,1,0:T(8,128)S(1)}, f32[1,5,8192]{2,1,0:T(8,128)S(1)}, u32[]{:S(2)}, u32[]{:S(2)}) collective-permute-start(f32[1,5,8192]{2,1,0:T(8,128)S(1)} %pad_maximum_fusion.refs_6_), channel_id=1, source_target_pairs={{1,0},{0,1},{3,2},{2,3},{5,4},{4,5},{7,6},{6,7},{9,8},{8,9},{11,10... | collective-permute-start | bytes 491528 | tf_op jit(solution)/shard_map/ppermute | solution.py:26
  10.2 5.3 %collective-permute-start.4 = (f32[1,2,8192]{2,1,0:T(2,128)S(1)}, f32[1,2,8192]{2,1,0:T(2,128)S(1)}, u32[]{:S(2)}, u32[]{:S(2)}) collective-permute-start(f32[1,2,8192]{2,1,0:T(2,128)S(1)} %copy-done.4), channel_id=1, source_target_pairs={{3,0},{2,1},{5,2},{4,3},{7,4},{6,5},{9,6},{8,7},{11,8},{10,9},{13,... | collective-permute-start | bytes 196616 | tf_op jit(solution)/shard_map/ppermute | solution.py:26
  15.6 0.7 %copy-done.7 = s32[64,5]{0,1:T(8,128)S(1)} copy-done((s32[64,5]{0,1:T(8,128)S(1)}, s32[64,5]{0,1:T(8,128)}, u32[]{:S(2)}) %copy-start.7) | copy-done | bytes 1304
  16.2 0.7 %copy.16.refs_1_ = s32[64,5]{1,0:T(8,128)} copy(s32[64,5]{0,1:T(8,128)S(1)} %copy-done.7) | data formatting | bytes 2560 | tf_op args[7]
  17.0 0.6 %fusion.2 = (s32[1]{0:T(128)}, s32[1]{0:T(128)}) fusion(s32[16]{0:T(128)S(1)} %copy-done.8, s32[]{:T(128)S(6)} %select_n.35, s32[]{:T(128)S(6)} %select_n.38), kind=kLoop, calls=%fused_computation.7 | loop fusion | bytes 24 | tf_op jit(solution)/shard_map/dynamic_slice | solution.py:303
  19.0 0.5 copy-done.10
  19.5 0.1 copy-done.9
  19.6 0.1 copy-done.2
  19.7 0.1 copy-done.3
  19.8 28.8 %tiles.1 = (f32[1,3,8192]{2,1,0:T(4,128)}, f32[1,128]{1,0:T(1,128)}) custom-call(s32[1]{0:T(128)} %bitcast.refs_0_, s32[64,5]{1,0:T(8,128)} %copy.16.refs_1_, f32[16]{0:T(128)} %refs_2_.1, f32[16]{0:T(128)} %refs_3_.1, f32[1,16384]{1,0:T(1,128)} %bitcast.5, s32[1,16384]{1,0:T(1,128)} %bitcast.6, f32[1,5,8192]{2,1,0:T(8,128)} %copy-done.5, ...), custom_call_target="tpu_custom_call" | custom-call | flops 262144000 | bytes 1310720 | tf_op jit(solution)/shard_map/tiles/pallas_call | solution.py:263
  48.6 0.6 %copy-done.12 = f32[1,128]{1,0:T(1,128)S(1)} copy-done((f32[1,128]{1,0:T(1,128)S(1)}, f32[1,128]{1,0:T(1,128)}, u32[]{:S(2)}) %copy-start.12) | copy-done | bytes 536
  49.2 0.1 collective-permute-start.5
  49.3 1.5 %fusion = (f32[1,3,8192]{2,1,0:T(4,128)S(1)}, f32[1,3,8192]{2,1,0:T(4,128)S(1)}) fusion(f32[1,8,8192]{2,1,0:T(8,128)} %copy-done.2, f32[1,8,8192]{2,1,0:T(8,128)} %copy-done.3, pred[]{:T(512)} %bitcast.4, pred[]{:T(512)} %bitcast.3, f32[1,3,8192]{2,0,1:T(1,128)S(1)} %copy-done.1, f32[1,3,8192]{2,0,1:T(1,128)S(1)} %copy-done), kind=kLoop, calls=%fused_computation.3 | loop fusion | flops 98304 | bytes 786434 | tf_op jit(solution)/shard_map/jit(_where)/select_n | solution.py:306
  50.8 0.7 %copy.19 = f32[1,3,8192]{2,0,1:T(1,128)} copy(f32[1,3,8192]{2,1,0:T(4,128)S(1)} %copy-done.6) | data formatting | bytes 196608
  51.5 0.7 %copy.20 = f32[1,3,8192]{2,0,1:T(1,128)} copy(f32[1,3,8192]{2,1,0:T(4,128)S(1)} %get-tuple-element.13) | data formatting | bytes 196608
  52.3 0.7 %copy.21 = f32[1,3,8192]{2,0,1:T(1,128)} copy(f32[1,3,8192]{2,1,0:T(4,128)S(1)} %get-tuple-element.12) | data formatting | bytes 196608
  53.0 0.5 add_multiply_fusion
  (26 shorter events, 0.1 us)
Async XLA Ops:
  0.6 1.0 %copy-start.1 = (f32[1,3,8192]{2,0,1:T(1,128)S(1)}, f32[1,3,8192]{2,0,1:T(1,128)}, u32[]{:S(2)}) copy-start(f32[1,3,8192]{2,0,1:T(1,128)} %param.10) | copy-start | bytes 294916
  1.7 0.8 %copy-start.4 = (f32[1,2,8192]{2,1,0:T(2,128)S(1)}, f32[1,2,8192]{2,1,0:T(2,128)}, u32[]{:S(2)}) copy-start(f32[1,2,8192]{2,1,0:T(2,128)} %param.11) | copy-start | bytes 196612
  2.6 16.3 %collective-permute-start.1 = (f32[1,8,8192]{2,1,0:T(8,128)S(1)}, f32[1,8,8192]{2,1,0:T(8,128)S(1)}, u32[]{:S(2)}, u32[]{:S(2)}) collective-permute-start(f32[1,8,8192]{2,1,0:T(8,128)S(1)} %pad_maximum_fusion.1), channel_id=1, source_target_pairs={{30,0},{31,1},{0,2},{1,3},{2,4},{3,5},{4,6},{5,7},{6,8},{7,9},{8,1... | collective-permute-start | bytes 786440 | tf_op jit(solution)/shard_map/ppermute | solution.py:26
  3.1 15.8 %collective-permute-start.3 = (f32[1,8,8192]{2,1,0:T(8,128)S(1)}, f32[1,8,8192]{2,1,0:T(8,128)S(1)}, u32[]{:S(2)}, u32[]{:S(2)}) collective-permute-start(f32[1,8,8192]{2,1,0:T(8,128)S(1)} %pad_maximum_fusion.1), channel_id=1, source_target_pairs={{2,0},{3,1},{4,2},{5,3},{6,4},{7,5},{8,6},{9,7},{10,8},{11,9},{12,... | collective-permute-start | bytes 786440 | tf_op jit(solution)/shard_map/ppermute | solution.py:26
  8.2 10.7 %copy-start.5 = (f32[1,5,8192]{2,1,0:T(8,128)}, f32[1,5,8192]{2,1,0:T(8,128)S(1)}, u32[]{:S(2)}) copy-start(f32[1,5,8192]{2,1,0:T(8,128)S(1)} %pad_maximum_fusion.refs_6_) | copy-start | bytes 491524
  8.2 10.7 %collective-permute-start = (f32[1,5,8192]{2,1,0:T(8,128)S(1)}, f32[1,5,8192]{2,1,0:T(8,128)S(1)}, u32[]{:S(2)}, u32[]{:S(2)}) collective-permute-start(f32[1,5,8192]{2,1,0:T(8,128)S(1)} %pad_maximum_fusion.refs_6_), channel_id=1, source_target_pairs={{1,0},{0,1},{3,2},{2,3},{5,4},{4,5},{7,6},{6,7},{9,8},{8,9},{11,10... | collective-permute-start | bytes 491528 | tf_op jit(solution)/shard_map/ppermute | solution.py:26
  10.2 8.6 %collective-permute-start.2 = (f32[1,2,8192]{2,1,0:T(2,128)S(1)}, f32[1,2,8192]{2,1,0:T(2,128)S(1)}, u32[]{:S(2)}, u32[]{:S(2)}) collective-permute-start(f32[1,2,8192]{2,1,0:T(2,128)S(1)} %copy-done.4), channel_id=1, source_target_pairs={{31,0},{30,1},{1,2},{0,3},{3,4},{2,5},{5,6},{4,7},{7,8},{6,9},{9,1... | collective-permute-start | bytes 196616 | tf_op jit(solution)/shard_map/ppermute | solution.py:26
  10.2 8.7 %collective-permute-start.4 = (f32[1,2,8192]{2,1,0:T(2,128)S(1)}, f32[1,2,8192]{2,1,0:T(2,128)S(1)}, u32[]{:S(2)}, u32[]{:S(2)}) collective-permute-start(f32[1,2,8192]{2,1,0:T(2,128)S(1)} %copy-done.4), channel_id=1, source_target_pairs={{3,0},{2,1},{5,2},{4,3},{7,4},{6,5},{9,6},{8,7},{11,8},{10,9},{13,... | collective-permute-start | bytes 196616 | tf_op jit(solution)/shard_map/ppermute | solution.py:26
  15.6 0.7 %copy-start.7 = (s32[64,5]{0,1:T(8,128)S(1)}, s32[64,5]{0,1:T(8,128)}, u32[]{:S(2)}) copy-start(s32[64,5]{0,1:T(8,128)} %param.16) | copy-start | bytes 3844
  16.2 0.7 %copy-start.8 = (s32[16]{0:T(128)S(1)}, s32[16]{0:T(128)}, u32[]{:S(2)}) copy-start(s32[16]{0:T(128)} %param.17) | copy-start | bytes 196
  18.9 0.6 %copy-start.10 = (f32[1,2,8192]{2,1,0:T(2,128)}, f32[1,2,8192]{2,1,0:T(2,128)S(1)}, u32[]{:S(2)}) copy-start(f32[1,2,8192]{2,1,0:T(2,128)S(1)} %collective-permute-done.2.refs_9_) | copy-start | bytes 196612
  18.9 0.6 %copy-start.11 = (f32[1,2,8192]{2,1,0:T(2,128)}, f32[1,2,8192]{2,1,0:T(2,128)S(1)}, u32[]{:S(2)}) copy-start(f32[1,2,8192]{2,1,0:T(2,128)S(1)} %collective-permute-done.4.refs_11_) | copy-start | bytes 196612
  18.9 0.7 %copy-start.9 = (f32[1,5,8192]{2,1,0:T(8,128)}, f32[1,5,8192]{2,1,0:T(8,128)S(1)}, u32[]{:S(2)}) copy-start(f32[1,5,8192]{2,1,0:T(8,128)S(1)} %collective-permute-done.refs_7_) | copy-start | bytes 491524
  18.9 0.8 %copy-start.2 = (f32[1,8,8192]{2,1,0:T(8,128)}, f32[1,8,8192]{2,1,0:T(8,128)S(1)}, u32[]{:S(2)}) copy-start(f32[1,8,8192]{2,1,0:T(8,128)S(1)} %collective-permute-done.1.refs_8_) | copy-start | bytes 786436
  18.9 0.8 %copy-start.3 = (f32[1,8,8192]{2,1,0:T(8,128)}, f32[1,8,8192]{2,1,0:T(8,128)S(1)}, u32[]{:S(2)}) copy-start(f32[1,8,8192]{2,1,0:T(8,128)S(1)} %collective-permute-done.3.refs_10_) | copy-start | bytes 786436
  19.8 29.6 %copy-start = (f32[1,3,8192]{2,0,1:T(1,128)S(1)}, f32[1,3,8192]{2,0,1:T(1,128)}, u32[]{:S(2)}) copy-start(f32[1,3,8192]{2,0,1:T(1,128)} %param.9) | copy-start | bytes 294916
  48.6 0.6 %copy-start.12 = (f32[1,128]{1,0:T(1,128)S(1)}, f32[1,128]{1,0:T(1,128)}, u32[]{:S(2)}) copy-start(f32[1,128]{1,0:T(1,128)} %get-tuple-element.6) | copy-start | bytes 1540
  49.2 3.8 %collective-permute-start.5 = (f32[1,128]{1,0:T(1,128)S(1)}, f32[1,128]{1,0:T(1,128)S(1)}, u32[]{:S(2)}, u32[]{:S(2)}) collective-permute-start(f32[1,128]{1,0:T(1,128)S(1)} %copy-done.12), channel_id=1, source_target_pairs={{1,0},{0,1},{3,2},{2,3},{5,4},{4,5},{7,6},{6,7},{9,8},{8,9},{11,10... | collective-permute-start | bytes 1544 | tf_op jit(solution)/shard_map/ppermute | solution.py:26
  49.3 1.5 %copy-start.6 = (f32[1,3,8192]{2,1,0:T(4,128)S(1)}, f32[1,3,8192]{2,1,0:T(4,128)}, u32[]{:S(2)}) copy-start(f32[1,3,8192]{2,1,0:T(4,128)} %get-tuple-element.9) | copy-start | bytes 294916

commit v2 on v1

v2 whole, which is shorter than its diff:
```python
import math
from functools import partial

import jax
import jax.numpy as jnp
from jax import lax
from jax.experimental import pallas as pl
from jax.experimental.pallas import tpu as pltpu
from jax.sharding import PartitionSpec as P

TILE = 128
DELTA_SOFT = 0.05
SUB = 16
DEPTH = 32
COLS = 2
UNROLL = 8
GROUP = 8
MESH = pl.DeviceIdType.MESH


def halved(x):
    high = x.astype(jnp.bfloat16)
    low = x - high.astype(jnp.float32)
    return jnp.concatenate([high, low.astype(jnp.bfloat16)], axis=1)


def rounded(x):
    return x.astype(jnp.bfloat16).astype(jnp.float32)


def tiles_kernel(
    parts, listed, near_ref, sigma_ref, eps_ref, accept_ref, charges_ref, types_ref, coords_ref, velocities_ref,
    coupling_ref, energy_ref, force_ref, new_coords_ref, new_velocities_ref, cols, near_feat, own_feat, lhs_e, lhs_f,
    far_coords, far_coupling, lam_coupling, lam_coords, lam_velocities, share, far_share,
    send_part, recv_part, send_lam, recv_lam, send_more, recv_more, *rest
):
    unroll = len(rest) // 2
    geos, sums = rest[:unroll], rest[unroll:]
    width = coords_ref.shape[2]
    atoms = cols.shape[1]
    row_tiles = width // TILE
    cycle = lax.axis_size("lam")
    replica, part = lax.axis_index("lam"), lax.axis_index("atom")
    first_tile = part * row_tiles
    upper, lower = lax.rem(replica + 1, cycle), lax.rem(replica + cycle - 1, cycle)

    def place(r, p):
        return {"lam": r, "atom": p}

    def copy(src, dst, send, recv, target):
        return pltpu.make_async_remote_copy(
            src_ref=src, dst_ref=dst, send_sem=send, recv_sem=recv, device_id=target, device_id_type=MESH
        )

    def partner(step):
        return place(replica, lax.rem(part + parts - step, parts))

    sides = (place(upper, part), place(lower, part))
    barrier = pltpu.get_barrier_semaphore()
    greeted = [partner(step) for step in range(1, parts)] + list(sides)
    for target in greeted:
        pl.semaphore_signal(barrier, inc=1, device_id=target, device_id_type=MESH)

    kinds = types_ref[...]
    radius = jnp.zeros(kinds.shape, jnp.float32)
    depth = jnp.zeros(kinds.shape, jnp.float32)
    for level in range(sigma_ref.shape[0]):
        here = kinds == level
        radius = jnp.where(here, sigma_ref[level], radius)
        depth = jnp.where(here, eps_ref[level], depth)
    cols[3:4, :] = 0.5 * radius
    base = 2.0 * jnp.sqrt(depth)
    for row in (11, 15):
        cols[row : row + 1, :] = jnp.zeros((1, atoms), jnp.float32)
    for h in range(3):
        cols[8 + h : 9 + h, :] = charges_ref[...]
        cols[12 + h : 13 + h, :] = base
    spans = []
    for step in range(parts):
        start = pl.multiple_of(lax.rem(part + step, parts) * width, TILE)
        spans.append(pl.ds(start, width))

    pl.semaphore_wait(barrier, len(greeted))
    far_c = [
        copy(coupling_ref, far_coupling.at[step - 1], send_part.at[0, step - 1], recv_part.at[0, step - 1], partner(step))
        for step in range(1, parts)
    ]
    far_x = [
        copy(coords_ref, far_coords.at[step - 1], send_part.at[1, step - 1], recv_part.at[1, step - 1], partner(step))
        for step in range(1, parts)
    ]
    near_c = [
        [
            copy(
                coupling_ref if step == 0 else far_coupling.at[step - 1],
                lam_coupling.at[side, step],
                send_lam.at[side, step],
                recv_lam.at[side, step],
                sides[side],
            )
            for step in range(parts)
        ]
        for side in range(2)
    ]
    swaps = [
        copy(src, dst.at[side], send_more.at[i, side], recv_more.at[i, side], sides[side])
        for side in range(2)
        for i, (src, dst) in enumerate(((coords_ref, lam_coords), (velocities_ref, lam_velocities)))
    ]
    for c in far_c:
        c.start()
    for side in range(2):
        near_c[side][0].start()
    for c in far_x:
        c.start()

    def set_coords(step, ref):
        for c in range(3):
            cols[c : c + 1, spans[step]] = ref[c] - 0.5

    def set_coupling(h, step, ref):
        for c, row in ((0, 8 + h), (1, 12 + h)):
            cols[row : row + 1, spans[step]] = cols[row : row + 1, spans[step]] * ref[c]

    set_coords(0, coords_ref)
    set_coupling(0, 0, coupling_ref)

    def rows_of(n):
        return lax.broadcasted_iota(jnp.int32, (8, n), 0)

    def base_rows(span):
        four = cols[0:4, span]
        return jnp.concatenate([four, four], axis=0)

    def thirds(x):
        high = rounded(x)
        low = x - high
        mid = rounded(low)
        return high, mid, low - mid

    def near_part(c):
        span = pl.ds(pl.multiple_of(c * TILE, TILE), TILE)
        sub = rows_of(TILE)
        quad = sub % 4
        f8 = base_rows(span)
        high, mid, low = thirds(f8)
        sign = jnp.where(quad == 3, 2.0, -2.0).astype(jnp.float32)
        square = f8 * f8
        norm = square[0:1] + square[1:2] + square[2:3]
        mixed = jnp.where(sub < 3, norm, square[3:4])
        nh, nm, nl = thirds(mixed)
        last = jnp.where(quad == 0, nh, jnp.where(quad == 1, nm, nl))
        last = jnp.where(sub == 3, nh, jnp.where(sub == 4, nm, last))
        last = jnp.where(sub >= 5, 1.0, last)
        feats = jnp.concatenate([high * sign, mid * sign, jnp.where(sub < 4, high, low) * sign, last], axis=0)
        near_feat[c] = feats.astype(jnp.bfloat16).T

    def near_half(step):
        offset = lax.rem(part + step, parts) * row_tiles

        def some(c, carry):
            for i in range(GROUP):
                near_part(offset + GROUP * c + i)
            return carry

        lax.fori_loop(0, row_tiles // GROUP, some, 0)

    def lhs_part(c):
        span = pl.ds(pl.multiple_of(c * TILE, TILE), TILE)
        sub = rows_of(TILE)
        quad = sub % 4
        f8 = base_rows(span)
        own8 = cols[8:16, span]
        oh = rounded(own8)
        lhs_e[c] = jnp.concatenate([oh, own8 - oh], axis=0).astype(jnp.bfloat16)
        pos = jnp.where(quad == 3, 1.0, f8)
        scale = jnp.where(sub < 4, own8[0:1], 6.0 * own8[4:5])
        wide = pos * scale
        wh = rounded(wide)
        lhs_f[c] = jnp.concatenate([wh, wide - wh], axis=0).astype(jnp.bfloat16)

    def lhs_parts(c, carry):
        for i in range(GROUP):
            lhs_part(GROUP * c + i)
        return carry

    def own_part(c):
        span = pl.ds(pl.multiple_of((first_tile + c) * TILE, TILE), TILE)
        sub = rows_of(TILE)
        quad = sub % 4
        f8 = base_rows(span)
        high, mid, low = thirds(f8)
        square = f8 * f8
        norm = square[0:1] + square[1:2] + square[2:3]
        first = jnp.where(sub < 4, high, mid)
        third = jnp.where(sub < 4, low, high)
        outs = []
        for which in range(COLS):
            const = (norm + DELTA_SOFT, norm + square[3:4], square[3:4])[which]
            ch, cm, cl = thirds(const)
            ones = sub < (3, 5, 5)[which]
            if which == 2:
                ones = (sub == 3) | (sub == 4)
            last = jnp.where(ones, 1.0, 0.0)
            last = jnp.where(sub == 5, ch, jnp.where(sub == 6, cm, jnp.where(sub == 7, cl, last)))
            keep = (quad != 3, quad <= 3, quad == 3)[which]
            a = jnp.where(keep, first, 0.0)
            outs.append(jnp.concatenate([a, a, jnp.where(keep, third, 0.0), last], axis=0))
        spot = pl.ds(pl.multiple_of(c * (COLS * TILE), TILE), COLS * TILE)
        own_feat[:, spot] = jnp.concatenate(outs, axis=1).astype(jnp.bfloat16)

    def own_parts(c, carry):
        for i in range(GROUP):
            own_part(GROUP * c + i)
        return carry

    lax.fori_loop(0, row_tiles // GROUP, own_parts, 0)
    near_half(0)
    for step in range(1, parts):
        far_c[step - 1].wait_recv()
        for side in range(2):
            near_c[side][step].start()
    for c in swaps:
        c.start()
    for step in range(1, parts):
        set_coupling(0, step, far_coupling.at[step - 1])
        far_x[step - 1].wait_recv()
        set_coords(step, far_coords.at[step - 1])
        near_half(step)
    for side, h in ((0, 1), (1, 2)):
        for step in range(parts):
            near_c[side][step].wait_recv()
            set_coupling(h, step, lam_coupling.at[side, step])
    lax.fori_loop(0, atoms // (GROUP * TILE), lhs_parts, 0)

    def geometry(t, s):
        spot = pl.ds(pl.multiple_of(t * (COLS * TILE), TILE), COLS * TILE)
        rhs = own_feat[:, spot]
        for k in range(listed):
            geos[s][k] = jnp.dot(near_feat[near_ref[k, t]], rhs, preferred_element_type=jnp.float32)

    def blocks(t, s):
        total = None
        for k in range(listed):
            invs, charge, ljs, well = [], [], [], []
            for b in range(TILE // SUB):
                rows = pl.ds(b * SUB, SUB)
                inv = lax.rsqrt(geos[s][k, rows, 0:TILE])
                charge.append(halved(inv * (inv * inv)))
                invs.append(inv.astype(jnp.bfloat16))
            for b in range(TILE // SUB):
                rows = pl.ds(b * SUB, SUB)
                both = geos[s][k, rows, TILE : 2 * TILE]
                root = lax.rsqrt(both)
                p = root * root
                if COLS == 3:
                    x = geos[s][k, rows, 2 * TILE : 3 * TILE] * p
                else:
                    x = ((both - geos[s][k, rows, 0:TILE]) + DELTA_SOFT) * p
                x3 = x * x * x
                low = x3 - 1.0
                ljs.append((x3 * low).astype(jnp.bfloat16))
                well.append(halved((x3 * p) * (x3 + low)))
            le = lhs_e[near_ref[k, t]]
            lf = lhs_f[near_ref[k, t]]
            fc = jnp.dot(lf, jnp.concatenate(charge, axis=0), preferred_element_type=jnp.float32)
            fw = jnp.dot(lf, jnp.concatenate(well, axis=0), preferred_element_type=jnp.float32)
            pairs = jnp.concatenate([jnp.concatenate(invs, axis=0), jnp.concatenate(ljs, axis=0)], axis=1)
            en = jnp.dot(le, pairs, preferred_element_type=jnp.float32)
            new = (fc, fw, en)
            total = new if total is None else tuple(x + y for x, y in zip(total, new))
        for i, x in enumerate(total):
            sums[s][i] = x

    def own_hits(t):
        hits = jnp.int32(0)
        for k in range(listed):
            away = near_ref[k, t] - (first_tile + t)
            hits = hits + 1 - jnp.minimum(away * away, 1)
        return jnp.full((8, TILE), hits, jnp.int32).astype(jnp.float32)

    def finish(t, s, carry):
        totals, selfs = carry
        own = first_tile + t
        own_span = pl.ds(pl.multiple_of(own * TILE, TILE), TILE)
        out_span = pl.ds(pl.multiple_of(t * TILE, TILE), TILE)
        sub = rows_of(TILE)
        quad = sub % 4
        mine = cols[8:16, own_span]
        fold = []
        for i in range(2):
            x = sums[s][i, 0:8] + sums[s][i, 8:16]
            fold.append(x[:, :TILE] + x[:, TILE:])
        en = sums[s][2, 0:8] + sums[s][2, 8:16]
        totals = totals + mine * jnp.where(sub < 4, en[:, :TILE], en[:, TILE:])
        selfs = selfs + own_hits(t) * (mine * mine)
        pull = jnp.where(sub < 4, fold[0] * mine[0:1], fold[1] * mine[4:5])
        pull = pull[0:4] + pull[4:8]
        force = cols[0:3, own_span] * pull[3:4] - pull[0:3]
        for c in range(3):
            force_ref[c, :, out_span] = force[c : c + 1]
        return totals, selfs

    def step(m, carry):
        for s in range(unroll):
            t = unroll * m + s
            before = (s - 1) % unroll
            carry = finish(jnp.maximum(t - 1, 0), before, carry)
            geometry(jnp.minimum(t + 1, row_tiles - 1), (s + 1) % unroll)
            blocks(t, s)
        return carry

    zero = jnp.zeros((8, TILE), jnp.float32)
    sums[unroll - 1][...] = jnp.zeros(sums[unroll - 1].shape, jnp.float32)
    geometry(0, 0)
    carry = lax.fori_loop(0, row_tiles // unroll, step, (zero, zero))
    first = cols[8:16, pl.ds(pl.multiple_of(first_tile * TILE, TILE), TILE)]
    totals, selfs = finish(row_tiles - 1, unroll - 1, carry)
    selfs = selfs - own_hits(0) * (first * first)
    soft = rounded(lax.rsqrt(jnp.full((8, TILE), DELTA_SOFT, jnp.float32)))
    sub = rows_of(TILE)
    share[...] = totals - jnp.where(sub < 4, selfs * soft, 0.0)

    for c in swaps:
        c.wait_recv()
    up = accept_ref[replica]
    low = accept_ref[lower]

    def swapped(out, ref, got):
        for c in range(3):
            up_flag = jnp.full((1, width), up, jnp.int32) == 1
            low_flag = jnp.full((1, width), low, jnp.int32) == 1
            out[c] = jnp.where(up_flag, got[1, c], jnp.where(low_flag, got[0, c], ref[c]))

    swapped(new_coords_ref, coords_ref, lam_coords)
    far_e = [
        copy(share, far_share.at[step - 1], send_part.at[2, step - 1], recv_part.at[2, step - 1], partner(step))
        for step in range(1, parts)
    ]
    for c in far_e:
        c.start()
    swapped(new_velocities_ref, velocities_ref, lam_velocities)
    for c in far_c + far_x + near_c[0] + near_c[1] + swaps:
        c.wait_send()
    for c in far_e:
        c.wait()
    both = share[...]
    if parts == 2:
        both = both + far_share[0]
    elif parts > 2:
        both = jnp.zeros_like(both)
        for p in range(parts):
            for step in range(parts):
                here = jnp.full((8, TILE), lax.rem(part + step, parts), jnp.int32) == p
                both = both + jnp.where(here, share[...] if step == 0 else far_share[step - 1], 0.0)
    lane1 = lax.broadcasted_iota(jnp.int32, (1, TILE), 1)
    line = jnp.zeros((1, TILE), jnp.float32)
    for h in range(3):
        value = jnp.sum(both[h : h + 1] + both[4 + h : 5 + h])
        line = jnp.where(lane1 == h, value * (0.5 / atoms), line)
    energy_ref[...] = line


def per_device(
    coords, velocities, coupling, charges, types, type_sigma, type_eps, near_tiles, accept
):
    parts, width = lax.axis_size("atom"), coords.shape[2]
    atoms = parts * width
    listed = near_tiles.shape[1]
    unroll = math.gcd(width // TILE, UNROLL)
    smem = pl.BlockSpec(memory_space=pltpu.SMEM)
    vmem = pl.BlockSpec(memory_space=pltpu.VMEM)
    f32, bf16, far = jnp.float32, jnp.bfloat16, max(parts - 1, 1)
    dma = pltpu.SemaphoreType.DMA
    rows = jax.ShapeDtypeStruct((3, 1, width), f32)
    line, force, new_coords, new_velocities = pl.pallas_call(
        partial(tiles_kernel, parts, listed),
        out_shape=(jax.ShapeDtypeStruct((1, TILE), f32), rows, rows, rows),
        in_specs=[smem] * 4 + [vmem] * 5,
        out_specs=(vmem,) * 4,
        scratch_shapes=[
            pltpu.VMEM((16, atoms), f32),
            pltpu.VMEM((atoms // TILE, TILE, DEPTH), bf16),
            pltpu.VMEM((DEPTH, COLS * width), bf16),
            pltpu.VMEM((atoms // TILE, 16, TILE), bf16),
            pltpu.VMEM((atoms // TILE, 16, TILE), bf16),
            pltpu.VMEM((far, 3, 1, width), f32),
            pltpu.VMEM((far, 2, 1, width), f32),
            pltpu.VMEM((2, parts, 2, 1, width), f32),
            pltpu.VMEM((2, 3, 1, width), f32),
            pltpu.VMEM((2, 3, 1, width), f32),
            pltpu.VMEM((8, TILE), f32),
            pltpu.VMEM((far, 8, TILE), f32),
            dma((3, far)),
            dma((3, far)),
            dma((2, parts)),
            dma((2, parts)),
            dma((2, 2)),
            dma((2, 2)),
        ]
        + [pltpu.VMEM((listed, TILE, COLS * TILE), f32)] * unroll
        + [pltpu.VMEM((3, 16, 2 * TILE), f32)] * unroll,
        compiler_params=pltpu.CompilerParams(collective_id=0, has_side_effects=True),
        name="tiles",
    )(
        near_tiles.T,
        type_sigma,
        type_eps,
        accept,
        charges.reshape(1, atoms),
        types.reshape(1, atoms),
        *(x.transpose(1, 0, 2) for x in (coords, velocities, coupling)),
    )
    return (line[:, :3], *(x.transpose(1, 0, 2) for x in (force, new_coords, new_velocities)))


def solution(mesh):
    split = P("lam", None, "atom")
    return jax.shard_map(
        per_device,
        mesh=mesh,
        in_specs=(split, split, split, P(), P(), P(), P(), P("atom", None), P()),
        out_specs=(P("lam", None), split, split, split),
        check_vma=False,
    )
```

time: 53.9 us -> 42.2 us (0.78)
  starting transfers between devices: 13 us -> 0 us
  Pallas kernels: 28.8 us -> 35.5 us
  other arithmetic: 2.12 us -> 0 us
  local copies, waits for them, and re-layouts: 7.5 us -> 5.77 us
  between operations: 2.09 us -> 0.65 us
    ppermute x6 -> x0, starting transfers between devices: 13 us -> none  [moved(): return lax.ppermute(x, ('lam', 'atom'), pairs)]
    pallas_call x1, Pallas kernels: 28.8 us -> 35.5 us  [per_device(): pl.pallas_call(partial(tiles_kernel, parts, listed), out_shape=(jax.Shape...]
    unnamed x32 -> x10, local copies, waits for them, and re-layouts: 6.91 us -> 4.26 us
    transpose x0 -> x1, local copies, waits for them, and re-layouts: none -> 1.51 us  [per_device(): x.transpose(1, 0, 2)]
    select_n x1 -> x0, other arithmetic: 1.46 us -> none  [per_device(): jnp.where(up, upper[:, 3:6], jnp.where(low, lower[:, 3:6], velocities))]
    dynamic_slice x1 -> x0, local copies, waits for them, and re-layouts: 0.59 us -> none  [per_device(): up = accept[replica] == 1]
  transfers between devices with their start and end apart: 6 -> 0, of which waited for: 0 -> 0; matrix products, arithmetic and copies ran while one was open for 9% -> 0% of each run, Pallas kernels for 0% -> 0%
where the time goes in v2:
time: 42.2 us; the launch traced here: 41.9 us
  Pallas kernels  35.5 us (84%)
  local copies, waits for them, and re-layouts  5.77 us (14%)
  between operations  0.65 us (2%)
    pallas_call x1, Pallas kernels, per_device(): pl.pallas_call(partial(tiles_kernel, parts, listed), out_shape=(jax.Shape...  35.5 us
    unnamed x10, local copies, waits for them, and re-layouts  4.26 us
    transpose x1, local copies, waits for them, and re-layouts, per_device(): x.transpose(1, 0, 2)  1.51 us

profile of v2, /device:TPU:0, one launch (start us, length us, event | category | flops | bytes accessed | tf_op | source)
XLA Modules:
  0.0 41.9 jit_solution(15237943019261183312)
XLA Ops:
  0.6 1.5 %transpose.24.coupling_ref = f32[2,1,8192]{2,1,0:T(1,128)} reshape(f32[1,2,8192]{2,1,0:T(2,128)} %param.11) | data formatting | bytes 131072 | tf_op jit(solution)/shard_map/transpose | solution.py:412
  2.1 35.5 %tiles.1 = (f32[1,128]{1,0:T(1,128)}, f32[3,1,8192]{2,1,0:T(1,128)}, f32[3,1,8192]{2,1,0:T(1,128)}, f32[3,1,8192]{2,1,0:T(1,128)}) custom-call(s32[5,64]{1,0:T(8,128)} %bitcast.16, f32[16]{0:T(128)} %sigma_ref.1, f32[16]{0:T(128)} %eps_ref.1, s32[16]{0:T(128)} %accept_ref.1, f32[1,16384]{1,0:T(1,128)} %bitcast.14, s32[1,16384]{1,0:T(1,128)} %bitcast.15, ...), custom_call_target="tpu_custom_call" | custom-call | tf_op jit(solution)/shard_map/tiles/pallas_call | solution.py:376
  37.7 0.0 copy-start.2
  37.7 0.6 %copy-done.2 = f32[1,128]{1,0:T(1,128)S(1)} copy-done((f32[1,128]{1,0:T(1,128)S(1)}, f32[1,128]{1,0:T(1,128)}, u32[]{:S(2)}) %copy-start.2) | copy-done | bytes 536
  38.3 0.5 %copy.17 = f32[1,3]{1,0:T(1,128)} copy(f32[1,3]{1,0:T(1,128)S(1)} %bitcast.17) | data formatting | bytes 24
  38.8 0.0 copy-start.1
  38.8 1.6 %copy.18 = f32[1,3,8192]{2,0,1:T(1,128)} copy(f32[1,3,8192]{2,0,1:T(1,128)} %bitcast.11) | data formatting | bytes 196608
  40.4 0.0 copy-done.1
  40.4 0.0 copy-start
  40.4 0.6 %copy.19 = f32[1,3,8192]{2,0,1:T(1,128)} copy(f32[1,3,8192]{2,0,1:T(1,128)S(1)} %bitcast.10) | data formatting | bytes 196608
  41.0 0.3 copy-done
  41.3 0.6 %copy.20 = f32[1,3,8192]{2,0,1:T(1,128)} copy(f32[1,3,8192]{2,0,1:T(1,128)S(1)} %bitcast.9) | data formatting | bytes 196608
Async XLA Ops:
  37.7 0.6 %copy-start.2 = (f32[1,128]{1,0:T(1,128)S(1)}, f32[1,128]{1,0:T(1,128)}, u32[]{:S(2)}) copy-start(f32[1,128]{1,0:T(1,128)} %get-tuple-element.8) | copy-start | bytes 1540
  38.8 1.6 %copy-start.1 = (f32[3,1,8192]{2,1,0:T(1,128)S(1)}, f32[3,1,8192]{2,1,0:T(1,128)}, u32[]{:S(2)}) copy-start(f32[3,1,8192]{2,1,0:T(1,128)} %get-tuple-element.10) | copy-start | bytes 294916
  40.4 0.9 %copy-start = (f32[3,1,8192]{2,1,0:T(1,128)S(1)}, f32[3,1,8192]{2,1,0:T(1,128)}, u32[]{:S(2)}) copy-start(f32[3,1,8192]{2,1,0:T(1,128)} %get-tuple-element.11) | copy-start | bytes 294916

commit v3 on v2

--- a/solution.py
+++ b/solution.py
@@ -29,8 +29,9 @@
 
 
 def tiles_kernel(
-    parts, listed, near_ref, sigma_ref, eps_ref, accept_ref, charges_ref, types_ref, coords_ref, velocities_ref,
-    coupling_ref, energy_ref, force_ref, new_coords_ref, new_velocities_ref, cols, near_feat, own_feat, lhs_e, lhs_f,
+    parts, listed, near_ref, sigma_ref, eps_ref, accept_ref, charges_hbm, types_hbm, coords_hbm,
+    velocities_hbm, coupling_hbm, energy_ref, force_out, new_coords_out, new_velocities_out, charges_ref, types_ref,
+    coords_ref, velocities_ref, coupling_ref, force_ref, new_coords_ref, new_velocities_ref, own_sem, out_sem, cols, near_feat, own_feat, lhs_e, lhs_f,
     far_coords, far_coupling, lam_coupling, lam_coords, lam_velocities, share, far_share,
     send_part, recv_part, send_lam, recv_lam, send_more, recv_more, *rest
 ):
@@ -61,6 +62,17 @@
     for target in greeted:
         pl.semaphore_signal(barrier, inc=1, device_id=target, device_id_type=MESH)
 
+    own_refs = (
+        (types_hbm, types_ref),
+        (coords_hbm, coords_ref),
+        (charges_hbm, charges_ref),
+        (coupling_hbm, coupling_ref),
+        (velocities_hbm, velocities_ref),
+    )
+    owned = [pltpu.make_async_copy(src, dst, own_sem.at[i]) for i, (src, dst) in enumerate(own_refs)]
+    for c in owned:
+        c.start()
+    owned[0].wait()
     kinds = types_ref[...]
     radius = jnp.zeros(kinds.shape, jnp.float32)
     depth = jnp.zeros(kinds.shape, jnp.float32)
@@ -72,6 +84,7 @@
     base = 2.0 * jnp.sqrt(depth)
     for row in (11, 15):
         cols[row : row + 1, :] = jnp.zeros((1, atoms), jnp.float32)
+    owned[2].wait()
     for h in range(3):
         cols[8 + h : 9 + h, :] = charges_ref[...]
         cols[12 + h : 13 + h, :] = base
@@ -80,49 +93,17 @@
         start = pl.multiple_of(lax.rem(part + step, parts) * width, TILE)
         spans.append(pl.ds(start, width))
 
-    pl.semaphore_wait(barrier, len(greeted))
-    far_c = [
-        copy(coupling_ref, far_coupling.at[step - 1], send_part.at[0, step - 1], recv_part.at[0, step - 1], partner(step))
-        for step in range(1, parts)
-    ]
-    far_x = [
-        copy(coords_ref, far_coords.at[step - 1], send_part.at[1, step - 1], recv_part.at[1, step - 1], partner(step))
-        for step in range(1, parts)
-    ]
-    near_c = [
-        [
-            copy(
-                coupling_ref if step == 0 else far_coupling.at[step - 1],
-                lam_coupling.at[side, step],
-                send_lam.at[side, step],
-                recv_lam.at[side, step],
-                sides[side],
-            )
-            for step in range(parts)
-        ]
-        for side in range(2)
-    ]
-    swaps = [
-        copy(src, dst.at[side], send_more.at[i, side], recv_more.at[i, side], sides[side])
-        for side in range(2)
-        for i, (src, dst) in enumerate(((coords_ref, lam_coords), (velocities_ref, lam_velocities)))
-    ]
-    for c in far_c:
-        c.start()
-    for side in range(2):
-        near_c[side][0].start()
-    for c in far_x:
-        c.start()
-
     def set_coords(step, ref):
         for c in range(3):
             cols[c : c + 1, spans[step]] = ref[c] - 0.5
 
     def set_coupling(h, step, ref):
         for c, row in ((0, 8 + h), (1, 12 + h)):
-            cols[row : row + 1, spans[step]] = cols[row : row + 1, spans[step]] * ref[c]
-
+            cols[row : row + 1, spans[step]] = cols[row : row + 1, spans[step]] * ref[0, c : c + 1]
+
+    owned[1].wait()
     set_coords(0, coords_ref)
+    owned[3].wait()
     set_coupling(0, 0, coupling_ref)
 
     def rows_of(n):
@@ -215,13 +196,45 @@
         return carry
 
     lax.fori_loop(0, row_tiles // GROUP, own_parts, 0)
+    pl.semaphore_wait(barrier, len(greeted))
+    far_c = [
+        copy(coupling_ref, far_coupling.at[step - 1], send_part.at[0, step - 1], recv_part.at[0, step - 1], partner(step))
+        for step in range(1, parts)
+    ]
+    far_x = [
+        copy(coords_ref, far_coords.at[step - 1], send_part.at[1, step - 1], recv_part.at[1, step - 1], partner(step))
+        for step in range(1, parts)
+    ]
+    near_c = [
+        [
+            copy(
+                coupling_ref if step == 0 else far_coupling.at[step - 1],
+                lam_coupling.at[side, step],
+                send_lam.at[side, step],
+                recv_lam.at[side, step],
+                sides[side],
+            )
+            for step in range(parts)
+        ]
+        for side in range(2)
+    ]
+    swaps = [
+        copy(src, dst.at[side], send_more.at[i, side], recv_more.at[i, side], sides[side])
+        for side in range(2)
+        for i, (src, dst) in enumerate(((coords_ref, lam_coords), (velocities_ref, lam_velocities)))
+    ]
+    for c in far_c:
+        c.start()
+    for side in range(2):
+        near_c[side][0].start()
+    for c in far_x:
+        c.start()
+
     near_half(0)
     for step in range(1, parts):
         far_c[step - 1].wait_recv()
         for side in range(2):
             near_c[side][step].start()
-    for c in swaps:
-        c.start()
     for step in range(1, parts):
         set_coupling(0, step, far_coupling.at[step - 1])
         far_x[step - 1].wait_recv()
@@ -231,6 +244,9 @@
         for step in range(parts):
             near_c[side][step].wait_recv()
             set_coupling(h, step, lam_coupling.at[side, step])
+    owned[4].wait()
+    for c in swaps:
+        c.start()
     lax.fori_loop(0, atoms // (GROUP * TILE), lhs_parts, 0)
 
     def geometry(t, s):
@@ -321,6 +337,12 @@
     sub = rows_of(TILE)
     share[...] = totals - jnp.where(sub < 4, selfs * soft, 0.0)
 
+    outs = [
+        pltpu.make_async_copy(src, dst, out_sem.at[i])
+        for i, (src, dst) in enumerate(
+            ((force_ref, force_out), (new_coords_ref, new_coords_out), (new_velocities_ref, new_velocities_out))
+        )
+    ]
     for c in swaps:
         c.wait_recv()
     up = accept_ref[replica]
@@ -339,7 +361,10 @@
     ]
     for c in far_e:
         c.start()
+    outs[0].start()
     swapped(new_velocities_ref, velocities_ref, lam_velocities)
+    outs[1].start()
+    outs[2].start()
     for c in far_c + far_x + near_c[0] + near_c[1] + swaps:
         c.wait_send()
     for c in far_e:
@@ -359,6 +384,15 @@
         value = jnp.sum(both[h : h + 1] + both[4 + h : 5 + h])
         line = jnp.where(lane1 == h, value * (0.5 / atoms), line)
     energy_ref[...] = line
+    for c in outs:
+        c.wait()
+
+
+def handed_on(line_ref, *refs):
+    half = (len(refs) - 1) // 2
+    refs[half][...] = line_ref[:, 0:3]
+    for src, dst in zip(refs[:half], refs[half + 1 :]):
+        dst[...] = src[...]
 
 
 def per_device(
@@ -370,23 +404,34 @@
     unroll = math.gcd(width // TILE, UNROLL)
     smem = pl.BlockSpec(memory_space=pltpu.SMEM)
     vmem = pl.BlockSpec(memory_space=pltpu.VMEM)
+    whole = pl.BlockSpec(memory_space=pl.ANY)
     f32, bf16, far = jnp.float32, jnp.bfloat16, max(parts - 1, 1)
     dma = pltpu.SemaphoreType.DMA
     rows = jax.ShapeDtypeStruct((3, 1, width), f32)
     line, force, new_coords, new_velocities = pl.pallas_call(
         partial(tiles_kernel, parts, listed),
         out_shape=(jax.ShapeDtypeStruct((1, TILE), f32), rows, rows, rows),
-        in_specs=[smem] * 4 + [vmem] * 5,
-        out_specs=(vmem,) * 4,
+        in_specs=[smem] * 4 + [whole] * 5,
+        out_specs=(vmem,) + (whole,) * 3,
         scratch_shapes=[
+            pltpu.VMEM((1, atoms), f32),
+            pltpu.VMEM((1, atoms), jnp.int32),
+            pltpu.VMEM((3, 1, width), f32),
+            pltpu.VMEM((3, 1, width), f32),
+            pltpu.VMEM((1, 2, width), f32),
+            pltpu.VMEM((3, 1, width), f32),
+            pltpu.VMEM((3, 1, width), f32),
+            pltpu.VMEM((3, 1, width), f32),
+            dma((5,)),
+            dma((3,)),
             pltpu.VMEM((16, atoms), f32),
             pltpu.VMEM((atoms // TILE, TILE, DEPTH), bf16),
             pltpu.VMEM((DEPTH, COLS * width), bf16),
             pltpu.VMEM((atoms // TILE, 16, TILE), bf16),
             pltpu.VMEM((atoms // TILE, 16, TILE), bf16),
             pltpu.VMEM((far, 3, 1, width), f32),
-            pltpu.VMEM((far, 2, 1, width), f32),
-            pltpu.VMEM((2, parts, 2, 1, width), f32),
+            pltpu.VMEM((far, 1, 2, width), f32),
+            pltpu.VMEM((2, parts, 1, 2, width), f32),
             pltpu.VMEM((2, 3, 1, width), f32),
             pltpu.VMEM((2, 3, 1, width), f32),
             pltpu.VMEM((8, TILE), f32),
@@ -409,9 +454,18 @@
         accept,
         charges.reshape(1, atoms),
         types.reshape(1, atoms),
-        *(x.transpose(1, 0, 2) for x in (coords, velocities, coupling)),
+        coords.transpose(1, 0, 2),
+        velocities.transpose(1, 0, 2),
+        coupling,
     )
-    return (line[:, :3], *(x.transpose(1, 0, 2) for x in (force, new_coords, new_velocities)))
+    energies, *results = pl.pallas_call(
+        handed_on,
+        out_shape=(jax.ShapeDtypeStruct((1, 3), f32), rows, rows, rows),
+        in_specs=[vmem] * 4,
+        out_specs=(vmem,) * 4,
+        name="handed_on",
+    )(line, force, new_coords, new_velocities)
+    return (energies, *(x.transpose(1, 0, 2) for x in results))
 
 
 def solution(mesh):

time: 42.2 us -> 38.2 us (0.905)
  local copies, waits for them, and re-layouts: 5.77 us -> 0 us
  Pallas kernels: 35.5 us -> 37.4 us
    unnamed x10 -> x0, local copies, waits for them, and re-layouts: 4.26 us -> none
    pallas_call x0 -> x1, Pallas kernels: none -> 1.71 us  [per_device(): pl.pallas_call(handed_on, out_shape=(jax.ShapeDtypeStruct((1, 3), f32), r...]
    transpose x1 -> x0, local copies, waits for them, and re-layouts: 1.51 us -> none  [per_device(): x.transpose(1, 0, 2)]
where the time goes in v3:
time: 38.2 us; the launch traced here: 38 us
  Pallas kernels  37.4 us (98%)
  between operations  0.64 us (2%)
    pallas_call x1, Pallas kernels, per_device(): pl.pallas_call(partial(tiles_kernel, parts, listed), out_shape=(jax.Shape...  35.7 us
    pallas_call x1, Pallas kernels, per_device(): pl.pallas_call(handed_on, out_shape=(jax.ShapeDtypeStruct((1, 3), f32), r...  1.71 us

profile of v3, /device:TPU:0, one launch (start us, length us, event | category | flops | bytes accessed | tf_op | source)
XLA Modules:
  0.0 38.0 jit_solution(3965228815762576476)
XLA Ops:
  0.6 35.7 %tiles.1 = (f32[1,128]{1,0:T(1,128)}, f32[3,1,8192]{2,1,0:T(1,128)}, f32[3,1,8192]{2,1,0:T(1,128)}, f32[3,1,8192]{2,1,0:T(1,128)}) custom-call(s32[5,64]{1,0:T(8,128)} %bitcast.12, f32[16]{0:T(128)} %sigma_ref.1, f32[16]{0:T(128)} %eps_ref.1, s32[16]{0:T(128)} %accept_ref.1, f32[1,16384]{1,0:T(1,128)} %bitcast.10, s32[1,16384]{1,0:T(1,128)} %bitcast.11, ...), custom_call_target="tpu_custom_call" | custom-call | tf_op jit(solution)/shard_map/tiles/pallas_call | solution.py:411
  36.3 1.7 %handed_on.1 = (f32[1,3]{1,0:T(1,128)}, f32[3,1,8192]{2,1,0:T(1,128)}, f32[3,1,8192]{2,1,0:T(1,128)}, f32[3,1,8192]{2,1,0:T(1,128)}) custom-call(f32[1,128]{1,0:T(1,128)} %get-tuple-element.12.line_ref, f32[3,1,8192]{2,1,0:T(1,128)} %get-tuple-element.13.refs_0_, f32[3,1,8192]{2,1,0:T(1,128)} %get-tuple-element.14.refs_1_, ...), custom_call_target="tpu_custom_call" | custom-call | tf_op jit(solution)/shard_map/handed_on/pallas_call | solution.py:461

commit v4 on v3

--- a/solution.py
+++ b/solution.py
@@ -13,8 +13,10 @@
 SUB = 16
 DEPTH = 32
 COLS = 2
+CHUNK = 5
 UNROLL = 8
 GROUP = 8
+WIDE = 16
 MESH = pl.DeviceIdType.MESH
 
 
@@ -29,8 +31,8 @@
 
 
 def tiles_kernel(
-    parts, listed, near_ref, sigma_ref, eps_ref, accept_ref, charges_hbm, types_hbm, coords_hbm,
-    velocities_hbm, coupling_hbm, energy_ref, force_out, new_coords_out, new_velocities_out, charges_ref, types_ref,
+    parts, listed, near_hbm, sigma_hbm, eps_hbm, accept_hbm, charges_hbm, types_hbm, coords_hbm,
+    velocities_hbm, coupling_hbm, energy_ref, force_out, new_coords_out, new_velocities_out, near_ref, sigma_ref, eps_ref, accept_ref, charges_ref, types_ref,
     coords_ref, velocities_ref, coupling_ref, force_ref, new_coords_ref, new_velocities_ref, own_sem, out_sem, cols, near_feat, own_feat, lhs_e, lhs_f,
     far_coords, far_coupling, lam_coupling, lam_coords, lam_velocities, share, far_share,
     send_part, recv_part, send_lam, recv_lam, send_more, recv_more, *rest
@@ -68,11 +70,17 @@
         (charges_hbm, charges_ref),
         (coupling_hbm, coupling_ref),
         (velocities_hbm, velocities_ref),
+        (sigma_hbm, sigma_ref),
+        (eps_hbm, eps_ref),
+        (near_hbm, near_ref),
+        (accept_hbm, accept_ref),
     )
     owned = [pltpu.make_async_copy(src, dst, own_sem.at[i]) for i, (src, dst) in enumerate(own_refs)]
     for c in owned:
         c.start()
     owned[0].wait()
+    owned[5].wait()
+    owned[6].wait()
     kinds = types_ref[...]
     radius = jnp.zeros(kinds.shape, jnp.float32)
     depth = jnp.zeros(kinds.shape, jnp.float32)
@@ -136,15 +144,17 @@
         feats = jnp.concatenate([high * sign, mid * sign, jnp.where(sub < 4, high, low) * sign, last], axis=0)
         near_feat[c] = feats.astype(jnp.bfloat16).T
 
+    wide = math.gcd(row_tiles, WIDE)
+
     def near_half(step):
         offset = lax.rem(part + step, parts) * row_tiles
 
         def some(c, carry):
-            for i in range(GROUP):
-                near_part(offset + GROUP * c + i)
+            for i in range(wide):
+                near_part(offset + wide * c + i)
             return carry
 
-        lax.fori_loop(0, row_tiles // GROUP, some, 0)
+        lax.fori_loop(0, row_tiles // wide, some, 0)
 
     def lhs_part(c):
         span = pl.ds(pl.multiple_of(c * TILE, TILE), TILE)
@@ -245,6 +255,8 @@
             near_c[side][step].wait_recv()
             set_coupling(h, step, lam_coupling.at[side, step])
     owned[4].wait()
+    owned[7].wait()
+    owned[8].wait()
     for c in swaps:
         c.start()
     lax.fori_loop(0, atoms // (GROUP * TILE), lhs_parts, 0)
@@ -256,35 +268,42 @@
             geos[s][k] = jnp.dot(near_feat[near_ref[k, t]], rhs, preferred_element_type=jnp.float32)
 
     def blocks(t, s):
-        total = None
-        for k in range(listed):
-            invs, charge, ljs, well = [], [], [], []
-            for b in range(TILE // SUB):
-                rows = pl.ds(b * SUB, SUB)
-                inv = lax.rsqrt(geos[s][k, rows, 0:TILE])
-                charge.append(halved(inv * (inv * inv)))
-                invs.append(inv.astype(jnp.bfloat16))
-            for b in range(TILE // SUB):
-                rows = pl.ds(b * SUB, SUB)
-                both = geos[s][k, rows, TILE : 2 * TILE]
-                root = lax.rsqrt(both)
-                p = root * root
-                if COLS == 3:
-                    x = geos[s][k, rows, 2 * TILE : 3 * TILE] * p
-                else:
+        total = [None] * 3
+
+        def add(i, x):
+            total[i] = x if total[i] is None else total[i] + x
+
+        def dot(x, y):
+            return jnp.dot(x, y, preferred_element_type=jnp.float32)
+
+        for first in range(0, listed, CHUNK):
+            ks = range(first, min(first + CHUNK, listed))
+            invs, ljs = [], []
+            lf = [lhs_f[near_ref[k, t]] for k in ks]
+            le = [lhs_e[near_ref[k, t]] for k in ks]
+            charge, well = [], []
+            for k in ks:
+                for b in range(TILE // SUB):
+                    rows = pl.ds(b * SUB, SUB)
+                    inv = lax.rsqrt(geos[s][k, rows, 0:TILE])
+                    charge.append(halved(inv * (inv * inv)))
+                    invs.append(inv.astype(jnp.bfloat16))
+            for k in ks:
+                for b in range(TILE // SUB):
+                    rows = pl.ds(b * SUB, SUB)
+                    both = geos[s][k, rows, TILE : 2 * TILE]
+                    root = lax.rsqrt(both)
+                    p = root * root
                     x = ((both - geos[s][k, rows, 0:TILE]) + DELTA_SOFT) * p
-                x3 = x * x * x
-                low = x3 - 1.0
-                ljs.append((x3 * low).astype(jnp.bfloat16))
-                well.append(halved((x3 * p) * (x3 + low)))
-            le = lhs_e[near_ref[k, t]]
-            lf = lhs_f[near_ref[k, t]]
-            fc = jnp.dot(lf, jnp.concatenate(charge, axis=0), preferred_element_type=jnp.float32)
-            fw = jnp.dot(lf, jnp.concatenate(well, axis=0), preferred_element_type=jnp.float32)
+                    x3 = x * x * x
+                    low = x3 - 1.0
+                    ljs.append((x3 * low).astype(jnp.bfloat16))
+                    well.append(halved((x3 * p) * (x3 + low)))
+            lfs = jnp.concatenate(lf, axis=1)
+            add(0, dot(lfs, jnp.concatenate(charge, axis=0)))
+            add(1, dot(lfs, jnp.concatenate(well, axis=0)))
             pairs = jnp.concatenate([jnp.concatenate(invs, axis=0), jnp.concatenate(ljs, axis=0)], axis=1)
-            en = jnp.dot(le, pairs, preferred_element_type=jnp.float32)
-            new = (fc, fw, en)
-            total = new if total is None else tuple(x + y for x, y in zip(total, new))
+            add(2, dot(jnp.concatenate(le, axis=1), pairs))
         for i, x in enumerate(total):
             sums[s][i] = x
 
@@ -402,7 +421,6 @@
     atoms = parts * width
     listed = near_tiles.shape[1]
     unroll = math.gcd(width // TILE, UNROLL)
-    smem = pl.BlockSpec(memory_space=pltpu.SMEM)
     vmem = pl.BlockSpec(memory_space=pltpu.VMEM)
     whole = pl.BlockSpec(memory_space=pl.ANY)
     f32, bf16, far = jnp.float32, jnp.bfloat16, max(parts - 1, 1)
@@ -411,9 +429,13 @@
     line, force, new_coords, new_velocities = pl.pallas_call(
         partial(tiles_kernel, parts, listed),
         out_shape=(jax.ShapeDtypeStruct((1, TILE), f32), rows, rows, rows),
-        in_specs=[smem] * 4 + [whole] * 5,
+        in_specs=[whole] * 9,
         out_specs=(vmem,) + (whole,) * 3,
         scratch_shapes=[
+            pltpu.SMEM((listed, width // TILE), jnp.int32),
+            pltpu.SMEM(type_sigma.shape, f32),
+            pltpu.SMEM(type_eps.shape, f32),
+            pltpu.SMEM(accept.shape, jnp.int32),
             pltpu.VMEM((1, atoms), f32),
             pltpu.VMEM((1, atoms), jnp.int32),
             pltpu.VMEM((3, 1, width), f32),
@@ -422,7 +444,7 @@
             pltpu.VMEM((3, 1, width), f32),
             pltpu.VMEM((3, 1, width), f32),
             pltpu.VMEM((3, 1, width), f32),
-            dma((5,)),
+            dma((9,)),
             dma((3,)),
             pltpu.VMEM((16, atoms), f32),
             pltpu.VMEM((atoms // TILE, TILE, DEPTH), bf16),

time: 38.2 us -> 36.7 us (0.961)
  Pallas kernels: 37.4 us -> 35.8 us
    pallas_call x1, Pallas kernels: 35.7 us -> 34.1 us  [per_device(): pl.pallas_call(partial(tiles_kernel, parts, listed), out_shape=(jax.Shape...]
where the time goes in v4:
time: 36.7 us; the launch traced here: 36.4 us
  Pallas kernels  35.8 us (98%)
  between operations  0.64 us (2%)
    pallas_call x1, Pallas kernels, per_device(): pl.pallas_call(partial(tiles_kernel, parts, listed), out_shape=(jax.Shape...  34.1 us
    pallas_call x1, Pallas kernels, per_device(): pl.pallas_call(handed_on, out_shape=(jax.ShapeDtypeStruct((1, 3), f32), r...  1.71 us

profile of v4, /device:TPU:0, one launch (start us, length us, event | category | flops | bytes accessed | tf_op | source)
XLA Modules:
  0.0 36.4 jit_solution(10702882151391149906)
XLA Ops:
  0.6 34.1 %tiles.1 = (f32[1,128]{1,0:T(1,128)}, f32[3,1,8192]{2,1,0:T(1,128)}, f32[3,1,8192]{2,1,0:T(1,128)}, f32[3,1,8192]{2,1,0:T(1,128)}) custom-call(s32[5,64]{1,0:T(8,128)} %bitcast.12, f32[16]{0:T(128)} %sigma_hbm.1, f32[16]{0:T(128)} %eps_hbm.1, s32[16]{0:T(128)} %accept_hbm.1, f32[1,16384]{1,0:T(1,128)} %bitcast.10, s32[1,16384]{1,0:T(1,128)} %bitcast.11, ...), custom_call_target="tpu_custom_call" | custom-call | tf_op jit(solution)/shard_map/tiles/pallas_call | solution.py:429
  34.7 1.7 %handed_on.1 = (f32[1,3]{1,0:T(1,128)}, f32[3,1,8192]{2,1,0:T(1,128)}, f32[3,1,8192]{2,1,0:T(1,128)}, f32[3,1,8192]{2,1,0:T(1,128)}) custom-call(f32[1,128]{1,0:T(1,128)} %get-tuple-element.12.line_ref, f32[3,1,8192]{2,1,0:T(1,128)} %get-tuple-element.13.refs_0_, f32[3,1,8192]{2,1,0:T(1,128)} %get-tuple-element.14.refs_1_, ...), custom_call_target="tpu_custom_call" | custom-call | tf_op jit(solution)/shard_map/handed_on/pallas_call | solution.py:483

commit v5 on v4

--- a/solution.py
+++ b/solution.py
@@ -14,7 +14,8 @@
 DEPTH = 32
 COLS = 2
 CHUNK = 5
-UNROLL = 8
+UNROLL = 16
+PIECES = 1
 GROUP = 8
 WIDE = 16
 MESH = pl.DeviceIdType.MESH
@@ -35,7 +36,7 @@
     velocities_hbm, coupling_hbm, energy_ref, force_out, new_coords_out, new_velocities_out, near_ref, sigma_ref, eps_ref, accept_ref, charges_ref, types_ref,
     coords_ref, velocities_ref, coupling_ref, force_ref, new_coords_ref, new_velocities_ref, own_sem, out_sem, cols, near_feat, own_feat, lhs_e, lhs_f,
     far_coords, far_coupling, lam_coupling, lam_coords, lam_velocities, share, far_share,
-    send_part, recv_part, send_lam, recv_lam, send_more, recv_more, *rest
+    send_part, recv_part, send_x, recv_x, send_lam, recv_lam, send_more, recv_more, *rest
 ):
     unroll = len(rest) // 2
     geos, sums = rest[:unroll], rest[unroll:]
@@ -76,144 +77,26 @@
         (accept_hbm, accept_ref),
     )
     owned = [pltpu.make_async_copy(src, dst, own_sem.at[i]) for i, (src, dst) in enumerate(own_refs)]
-    for c in owned:
-        c.start()
-    owned[0].wait()
-    owned[5].wait()
-    owned[6].wait()
-    kinds = types_ref[...]
-    radius = jnp.zeros(kinds.shape, jnp.float32)
-    depth = jnp.zeros(kinds.shape, jnp.float32)
-    for level in range(sigma_ref.shape[0]):
-        here = kinds == level
-        radius = jnp.where(here, sigma_ref[level], radius)
-        depth = jnp.where(here, eps_ref[level], depth)
-    cols[3:4, :] = 0.5 * radius
-    base = 2.0 * jnp.sqrt(depth)
-    for row in (11, 15):
-        cols[row : row + 1, :] = jnp.zeros((1, atoms), jnp.float32)
-    owned[2].wait()
-    for h in range(3):
-        cols[8 + h : 9 + h, :] = charges_ref[...]
-        cols[12 + h : 13 + h, :] = base
-    spans = []
-    for step in range(parts):
-        start = pl.multiple_of(lax.rem(part + step, parts) * width, TILE)
-        spans.append(pl.ds(start, width))
-
-    def set_coords(step, ref):
-        for c in range(3):
-            cols[c : c + 1, spans[step]] = ref[c] - 0.5
-
-    def set_coupling(h, step, ref):
-        for c, row in ((0, 8 + h), (1, 12 + h)):
-            cols[row : row + 1, spans[step]] = cols[row : row + 1, spans[step]] * ref[0, c : c + 1]
-
+    for i in (3, 1, 0, 2, 5, 6, 4, 7, 8):
+        owned[i].start()
+    owned[3].wait()
     owned[1].wait()
-    set_coords(0, coords_ref)
-    owned[3].wait()
-    set_coupling(0, 0, coupling_ref)
-
-    def rows_of(n):
-        return lax.broadcasted_iota(jnp.int32, (8, n), 0)
-
-    def base_rows(span):
-        four = cols[0:4, span]
-        return jnp.concatenate([four, four], axis=0)
-
-    def thirds(x):
-        high = rounded(x)
-        low = x - high
-        mid = rounded(low)
-        return high, mid, low - mid
-
-    def near_part(c):
-        span = pl.ds(pl.multiple_of(c * TILE, TILE), TILE)
-        sub = rows_of(TILE)
-        quad = sub % 4
-        f8 = base_rows(span)
-        high, mid, low = thirds(f8)
-        sign = jnp.where(quad == 3, 2.0, -2.0).astype(jnp.float32)
-        square = f8 * f8
-        norm = square[0:1] + square[1:2] + square[2:3]
-        mixed = jnp.where(sub < 3, norm, square[3:4])
-        nh, nm, nl = thirds(mixed)
-        last = jnp.where(quad == 0, nh, jnp.where(quad == 1, nm, nl))
-        last = jnp.where(sub == 3, nh, jnp.where(sub == 4, nm, last))
-        last = jnp.where(sub >= 5, 1.0, last)
-        feats = jnp.concatenate([high * sign, mid * sign, jnp.where(sub < 4, high, low) * sign, last], axis=0)
-        near_feat[c] = feats.astype(jnp.bfloat16).T
-
-    wide = math.gcd(row_tiles, WIDE)
-
-    def near_half(step):
-        offset = lax.rem(part + step, parts) * row_tiles
-
-        def some(c, carry):
-            for i in range(wide):
-                near_part(offset + wide * c + i)
-            return carry
-
-        lax.fori_loop(0, row_tiles // wide, some, 0)
-
-    def lhs_part(c):
-        span = pl.ds(pl.multiple_of(c * TILE, TILE), TILE)
-        sub = rows_of(TILE)
-        quad = sub % 4
-        f8 = base_rows(span)
-        own8 = cols[8:16, span]
-        oh = rounded(own8)
-        lhs_e[c] = jnp.concatenate([oh, own8 - oh], axis=0).astype(jnp.bfloat16)
-        pos = jnp.where(quad == 3, 1.0, f8)
-        scale = jnp.where(sub < 4, own8[0:1], 6.0 * own8[4:5])
-        wide = pos * scale
-        wh = rounded(wide)
-        lhs_f[c] = jnp.concatenate([wh, wide - wh], axis=0).astype(jnp.bfloat16)
-
-    def lhs_parts(c, carry):
-        for i in range(GROUP):
-            lhs_part(GROUP * c + i)
-        return carry
-
-    def own_part(c):
-        span = pl.ds(pl.multiple_of((first_tile + c) * TILE, TILE), TILE)
-        sub = rows_of(TILE)
-        quad = sub % 4
-        f8 = base_rows(span)
-        high, mid, low = thirds(f8)
-        square = f8 * f8
-        norm = square[0:1] + square[1:2] + square[2:3]
-        first = jnp.where(sub < 4, high, mid)
-        third = jnp.where(sub < 4, low, high)
-        outs = []
-        for which in range(COLS):
-            const = (norm + DELTA_SOFT, norm + square[3:4], square[3:4])[which]
-            ch, cm, cl = thirds(const)
-            ones = sub < (3, 5, 5)[which]
-            if which == 2:
-                ones = (sub == 3) | (sub == 4)
-            last = jnp.where(ones, 1.0, 0.0)
-            last = jnp.where(sub == 5, ch, jnp.where(sub == 6, cm, jnp.where(sub == 7, cl, last)))
-            keep = (quad != 3, quad <= 3, quad == 3)[which]
-            a = jnp.where(keep, first, 0.0)
-            outs.append(jnp.concatenate([a, a, jnp.where(keep, third, 0.0), last], axis=0))
-        spot = pl.ds(pl.multiple_of(c * (COLS * TILE), TILE), COLS * TILE)
-        own_feat[:, spot] = jnp.concatenate(outs, axis=1).astype(jnp.bfloat16)
-
-    def own_parts(c, carry):
-        for i in range(GROUP):
-            own_part(GROUP * c + i)
-        return carry
-
-    lax.fori_loop(0, row_tiles // GROUP, own_parts, 0)
     pl.semaphore_wait(barrier, len(greeted))
     far_c = [
         copy(coupling_ref, far_coupling.at[step - 1], send_part.at[0, step - 1], recv_part.at[0, step - 1], partner(step))
         for step in range(1, parts)
     ]
+    bit = width // PIECES
     far_x = [
-        copy(coords_ref, far_coords.at[step - 1], send_part.at[1, step - 1], recv_part.at[1, step - 1], partner(step))
+        copy(
+            coords_ref.at[:, :, pl.ds(p * bit, bit)],
+            far_coords.at[step - 1, :, :, pl.ds(p * bit, bit)],
+            send_x.at[p, step - 1],
+            recv_x.at[p, step - 1],
+            partner(step),
+        )
         for step in range(1, parts)
+        for p in range(PIECES)
     ]
     near_c = [
         [
@@ -240,6 +123,133 @@
     for c in far_x:
         c.start()
 
+    owned[0].wait()
+    owned[5].wait()
+    owned[6].wait()
+    kinds = types_ref[...]
+    radius = jnp.zeros(kinds.shape, jnp.float32)
+    depth = jnp.zeros(kinds.shape, jnp.float32)
+    for level in range(sigma_ref.shape[0]):
+        here = kinds == level
+        radius = jnp.where(here, sigma_ref[level], radius)
+        depth = jnp.where(here, eps_ref[level], depth)
+    cols[3:4, :] = 0.5 * radius
+    base = 2.0 * jnp.sqrt(depth)
+    for row in (11, 15):
+        cols[row : row + 1, :] = jnp.zeros((1, atoms), jnp.float32)
+    owned[2].wait()
+    for h in range(3):
+        cols[8 + h : 9 + h, :] = charges_ref[...]
+        cols[12 + h : 13 + h, :] = base
+    spans = []
+    for step in range(parts):
+        start = pl.multiple_of(lax.rem(part + step, parts) * width, TILE)
+        spans.append(pl.ds(start, width))
+
+    def set_coords(step, ref):
+        for c in range(3):
+            cols[c : c + 1, spans[step]] = ref[c] - 0.5
+
+    def set_coupling(h, step, ref):
+        for c, row in ((0, 8 + h), (1, 12 + h)):
+            cols[row : row + 1, spans[step]] = cols[row : row + 1, spans[step]] * ref[0, c : c + 1]
+
+    set_coords(0, coords_ref)
+    set_coupling(0, 0, coupling_ref)
+
+    def rows_of(n):
+        return lax.broadcasted_iota(jnp.int32, (8, n), 0)
+
+    def base_rows(span):
+        four = cols[0:4, span]
+        return jnp.concatenate([four, four], axis=0)
+
+    def thirds(x):
+        high = rounded(x)
+        low = x - high
+        mid = rounded(low)
+        return high, mid, low - mid
+
+    def near_part(c):
+        span = pl.ds(pl.multiple_of(c * TILE, TILE), TILE)
+        sub = rows_of(TILE)
+        quad = sub % 4
+        f8 = base_rows(span)
+        high, mid, low = thirds(f8)
+        sign = jnp.where(quad == 3, 2.0, -2.0).astype(jnp.float32)
+        square = f8 * f8
+        norm = square[0:1] + square[1:2] + square[2:3]
+        mixed = jnp.where(sub < 3, norm, square[3:4])
+        nh, nm, nl = thirds(mixed)
+        last = jnp.where(quad == 0, nh, jnp.where(quad == 1, nm, nl))
+        last = jnp.where(sub == 3, nh, jnp.where(sub == 4, nm, last))
+        last = jnp.where(sub >= 5, 1.0, last)
+        feats = jnp.concatenate([high * sign, mid * sign, jnp.where(sub < 4, high, low) * sign, last], axis=0)
+        near_feat[c] = feats.astype(jnp.bfloat16).T
+
+    wide = math.gcd(row_tiles // PIECES, WIDE)
+
+    def near_half(step, piece=0, pieces=1):
+        count = row_tiles // pieces
+        offset = lax.rem(part + step, parts) * row_tiles + piece * count
+
+        def some(c, carry):
+            for i in range(wide):
+                near_part(offset + wide * c + i)
+            return carry
+
+        lax.fori_loop(0, count // wide, some, 0)
+
+    def lhs_part(c):
+        span = pl.ds(pl.multiple_of(c * TILE, TILE), TILE)
+        sub = rows_of(TILE)
+        quad = sub % 4
+        f8 = base_rows(span)
+        own8 = cols[8:16, span]
+        oh = rounded(own8)
+        lhs_e[c] = jnp.concatenate([oh, own8 - oh], axis=0).astype(jnp.bfloat16)
+        pos = jnp.where(quad == 3, 1.0, f8)
+        scale = jnp.where(sub < 4, own8[0:1], 6.0 * own8[4:5])
+        wide = pos * scale
+        wh = rounded(wide)
+        lhs_f[c] = jnp.concatenate([wh, wide - wh], axis=0).astype(jnp.bfloat16)
+
+    def lhs_parts(c, carry):
+        for i in range(GROUP):
+            lhs_part(GROUP * c + i)
+        return carry
+
+    def own_part(c):
+        span = pl.ds(pl.multiple_of((first_tile + c) * TILE, TILE), TILE)
+        sub = rows_of(TILE)
+        quad = sub % 4
+        f8 = base_rows(span)
+        high, mid, low = thirds(f8)
+        square = f8 * f8
+        norm = square[0:1] + square[1:2] + square[2:3]
+        first = jnp.where(sub < 4, high, mid)
+        third = jnp.where(sub < 4, low, high)
+        outs = []
+        for which in range(COLS):
+            const = (norm + DELTA_SOFT, norm + square[3:4], square[3:4])[which]
+            ch, cm, cl = thirds(const)
+            ones = sub < (3, 5, 5)[which]
+            if which == 2:
+                ones = (sub == 3) | (sub == 4)
+            last = jnp.where(ones, 1.0, 0.0)
+            last = jnp.where(sub == 5, ch, jnp.where(sub == 6, cm, jnp.where(sub == 7, cl, last)))
+            keep = (quad != 3, quad <= 3, quad == 3)[which]
+            a = jnp.where(keep, first, 0.0)
+            outs.append(jnp.concatenate([a, a, jnp.where(keep, third, 0.0), last], axis=0))
+        spot = pl.ds(pl.multiple_of(c * (COLS * TILE), TILE), COLS * TILE)
+        own_feat[:, spot] = jnp.concatenate(outs, axis=1).astype(jnp.bfloat16)
+
+    def own_parts(c, carry):
+        for i in range(GROUP):
+            own_part(GROUP * c + i)
+        return carry
+
+    lax.fori_loop(0, row_tiles // GROUP, own_parts, 0)
     near_half(0)
     for step in range(1, parts):
         far_c[step - 1].wait_recv()
@@ -247,9 +257,12 @@
             near_c[side][step].start()
     for step in range(1, parts):
         set_coupling(0, step, far_coupling.at[step - 1])
-        far_x[step - 1].wait_recv()
-        set_coords(step, far_coords.at[step - 1])
-        near_half(step)
+        for p in range(PIECES):
+            far_x[(step - 1) * PIECES + p].wait_recv()
+            start = pl.multiple_of(lax.rem(part + step, parts) * width + p * bit, TILE)
+            for c in range(3):
+                cols[c : c + 1, pl.ds(start, bit)] = far_coords[step - 1, c, :, pl.ds(p * bit, bit)] - 0.5
+            near_half(step, p, PIECES)
     for side, h in ((0, 1), (1, 2)):
         for step in range(parts):
             near_c[side][step].wait_recv()
@@ -460,6 +473,8 @@
             pltpu.VMEM((far, 8, TILE), f32),
             dma((3, far)),
             dma((3, far)),
+            dma((PIECES, far)),
+            dma((PIECES, far)),
             dma((2, parts)),
             dma((2, parts)),
             dma((2, 2)),

time: 36.7 us -> 35.8 us (0.975)
  Pallas kernels: 35.8 us -> 35 us
    pallas_call x1, Pallas kernels: 34.1 us -> 33.2 us  [per_device(): pl.pallas_call(partial(tiles_kernel, parts, listed), out_shape=(jax.Shape...]
where the time goes in v5:
time: 35.8 us; the launch traced here: 35.6 us
  Pallas kernels  35 us (98%)
  between operations  0.64 us (2%)
    pallas_call x1, Pallas kernels, per_device(): pl.pallas_call(partial(tiles_kernel, parts, listed), out_shape=(jax.Shape...  33.2 us
    pallas_call x1, Pallas kernels, per_device(): pl.pallas_call(handed_on, out_shape=(jax.ShapeDtypeStruct((1, 3), f32), r...  1.71 us

profile of v5, /device:TPU:0, one launch (start us, length us, event | category | flops | bytes accessed | tf_op | source)
XLA Modules:
  0.0 35.6 jit_solution(10788180131220388180)
XLA Ops:
  0.6 33.2 %tiles.1 = (f32[1,128]{1,0:T(1,128)}, f32[3,1,8192]{2,1,0:T(1,128)}, f32[3,1,8192]{2,1,0:T(1,128)}, f32[3,1,8192]{2,1,0:T(1,128)}) custom-call(s32[5,64]{1,0:T(8,128)} %bitcast.12, f32[16]{0:T(128)} %sigma_hbm.1, f32[16]{0:T(128)} %eps_hbm.1, s32[16]{0:T(128)} %accept_hbm.1, f32[1,16384]{1,0:T(1,128)} %bitcast.10, s32[1,16384]{1,0:T(1,128)} %bitcast.11, ...), custom_call_target="tpu_custom_call" | custom-call | tf_op jit(solution)/shard_map/tiles/pallas_call | solution.py:442
  33.9 1.7 %handed_on.1 = (f32[1,3]{1,0:T(1,128)}, f32[3,1,8192]{2,1,0:T(1,128)}, f32[3,1,8192]{2,1,0:T(1,128)}, f32[3,1,8192]{2,1,0:T(1,128)}) custom-call(f32[1,128]{1,0:T(1,128)} %get-tuple-element.12.line_ref, f32[3,1,8192]{2,1,0:T(1,128)} %get-tuple-element.13.refs_0_, f32[3,1,8192]{2,1,0:T(1,128)} %get-tuple-element.14.refs_1_, ...), custom_call_target="tpu_custom_call" | custom-call | tf_op jit(solution)/shard_map/handed_on/pallas_call | solution.py:498
